TPU v7x, 32 devices: a whole 2x2x4 slice. The times are simulated.
32 devices in a mesh: row: 8 (over z, y), col: 4 (over x, core).
Axes of the slice: x: 2, y: 2, z: 4, core: 2. Of those that a mesh axis runs over, the one named last changes fastest.
Arguments:
- tracer: float32 [128, 128, 512], P(None, 'row', 'col'), may hold values from -6 to 6
- symbol_x: float32 [128], replicated, may hold values from 0.3 to 3
- symbol_y: float32 [128], replicated, may hold values from 0.3 to 3
- symbol_z: float32 [512], replicated, may hold values from 0.3 to 3
Outputs:
- spectrum: float32 [128, 128, 512], P('row', 'col')
All inputs are finite; a program needn't handle non-finite values.
Results may differ from a plain program's by a relative error of at most 0.000075.
Values sent between devices are 32-bit elements; how exact they have to be, the bound alone decides.
No kernel may reach another device: no remote copies, remote signals or barrier semaphores. Data moves between devices by JAX's collectives and lax.ppermute only.
A program may use at most 64 MiB of HBM per device.

v0:
```python
import jax
import jax.numpy as jnp
from jax import lax
from jax.sharding import PartitionSpec as P


def transform_table(count):
    rank = jnp.arange(count)
    angle = (
        jnp.pi
        / (count + 1)
        * ((rank[:, None] + 1) * (rank[None, :] + 1) % (2 * count + 2)).astype(jnp.float32)
    )
    return jnp.sin(angle) * (2.0 / (count + 1)) ** 0.5


def to_modes(values, dim):
    moved = jnp.tensordot(
        values,
        transform_table(values.shape[dim]),
        axes=([dim], [0]),
        precision=lax.Precision.HIGHEST,
    )
    return jnp.moveaxis(moved, -1, dim)


def per_device(tracer, symbol_x, symbol_y, symbol_z):
    part_values = tracer
    part_values = to_modes(part_values, 0)
    part_values = lax.all_to_all(part_values, "row", split_axis=0, concat_axis=1, tiled=True)
    part_values = to_modes(part_values, 1)
    local_values = part_values
    local_values = lax.all_to_all(local_values, "col", split_axis=1, concat_axis=2, tiled=True)
    local_values = to_modes(local_values, 2)
    share_x = local_values.shape[0]
    part_x = lax.dynamic_slice_in_dim(symbol_x, lax.axis_index("row") * share_x, share_x)
    share_y = local_values.shape[1]
    part_y = lax.dynamic_slice_in_dim(symbol_y, lax.axis_index("col") * share_y, share_y)
    symbol = part_x[:, None, None] + part_y[None, :, None] + symbol_z[None, None, :]
    local_values = local_values * ((1.0 - 0.2 * symbol) / (1.0 + 0.2 * symbol))
    return local_values


def solution(mesh):
    in_specs = (P(None, "row", "col"), P(), P(), P())
    out_specs = P("row", "col", None)
    return jax.shard_map(
        per_device, mesh=mesh, in_specs=in_specs, out_specs=out_specs, check_vma=False
    )
```

profile of v0, /device:TPU:0, one launch (start us, length us, event | category | flops | bytes accessed | tf_op | source)
XLA Modules:
  0.0 66.0 jit_solution(14999294112049493810)
XLA Ops:
  0.0 0.0 copy-start
  0.0 1.2 %copy-done = f32[128,16,128]{2,1,0:T(8,128)S(1)} copy-done((f32[128,16,128]{2,1,0:T(8,128)S(1)}, f32[128,16,128]{2,1,0:T(8,128)}, u32[]{:S(2)}) %copy-start) | copy-done | bytes 1048600
  1.2 1.6 %fusion.6 = f32[128,16,128]{2,0,1:T(8,128)S(1)} fusion(f32[128,16,128]{2,1,0:T(8,128)S(1)} %copy-done, s32[128]{0:T(128)S(1)} %iota_add_fusion.1), kind=kOutput, calls=%fused_computation.8 | convolution fusion | flops 402817024 | bytes 2097664 | tf_op jit(solution)/shard_map/dot_general | solution.py:18
  2.8 0.6 copy.24
  3.5 32.9 %all_to_all.36 = f32[128,16,128]{2,1,0:T(8,128)S(1)} all-to-all(f32[128,16,128]{2,1,0:T(8,128)S(1)} %copy.24), channel_id=1, replica_groups=mesh['row'=8,'col'=4] {'row'}, dimensions={0} | all-to-all | bytes 2097152 | tf_op jit(solution)/shard_map/all_to_all | solution.py:30
  36.3 0.1 copy.25
  36.4 2.0 %convolution_bitcast_fusion = f32[16,128,128]{1,2,0:T(8,128)S(1)} fusion(f32[16,128,128]{2,1,0:T(8,128)S(1)} %bitcast.21, s32[128]{0:T(128)S(1)} %iota_add_fusion.1), kind=kOutput, calls=%fused_computation.2 | convolution fusion | flops 402817024 | bytes 2097664 | tf_op jit(solution)/shard_map/dot_general | solution.py:18
  38.4 1.4 %copy.27 = f32[16,128,128]{2,0,1:T(8,128)} copy(f32[16,128,128]{1,2,0:T(8,128)S(1)} %convolution_bitcast_fusion) | data formatting | bytes 2097152 | tf_op jit(solution)/shard_map/transpose | solution.py:24
  39.8 3.7 %all-to-all-start.1 = ((f32[16,128,128]{2,0,1:T(8,128)}), f32[16,128,128]{2,0,1:T(8,128)S(1)}, u32[]{:S(2)}, u32[]{:S(2)}) async-start(f32[16,128,128]{2,0,1:T(8,128)} %copy.27), calls=%async_computation.1 | async-start | bytes 2097152 | tf_op jit(solution)/shard_map/all_to_all | solution.py:33
  43.5 0.0 copy-start.2
  43.5 0.6 copy-done.2
  44.2 0.1 dynamic_slice.7
  44.2 0.0 copy-start.3
  44.2 0.7 copy-done.3
  44.9 0.1 dynamic_slice.6
  45.0 0.1 broadcast_add_fusion
  45.0 12.7 %all-to-all-done.1 = f32[16,128,128]{2,0,1:T(8,128)S(1)} async-done(((f32[16,128,128]{2,0,1:T(8,128)}), f32[16,128,128]{2,0,1:T(8,128)S(1)}, u32[]{:S(2)}, u32[]{:S(2)}) %all-to-all-start.1) | async-done | bytes 1048608 | tf_op jit(solution)/shard_map/all_to_all | solution.py:33
  57.7 0.7 %copy.29 = f32[16,32,4,128]{3,2,1,0:T(4,128)S(1)} copy(f32[16,32,4,128]{3,0,1,2:T(8,128)S(1)} %bitcast.19) | data formatting | bytes 2097152 | tf_op jit(solution)/shard_map/all_to_all | solution.py:33
  58.4 0.0 copy-start.1
  58.4 0.4 all_to_all.33
  58.8 0.2 copy-done.1
  59.1 7.0 %convolution_multiply_fusion = f32[16,32,512]{2,1,0:T(8,128)} fusion(f32[16,32,512]{2,1,0:T(8,128)S(1)} %all_to_all.33, f32[512]{0:T(512)S(1)} %copy-done.1, f32[16,32]{1,0:T(8,128)S(1)} %broadcast_add_fusion, s32[512]{0:T(512)S(1)} %iota_add_fusion), kind=kOutput, calls=%fused_computation.1 | convolution fusion | flops 1614807040 | bytes 2103296 | tf_op jit(solution)/shard_map/dot_general | solution.py:18
  (2 shorter events, 0.0 us)
Async XLA Ops:
  0.0 1.2 %copy-start = (f32[128,16,128]{2,1,0:T(8,128)S(1)}, f32[128,16,128]{2,1,0:T(8,128)}, u32[]{:S(2)}) copy-start(f32[128,16,128]{2,1,0:T(8,128)} %param.4) | copy-start | bytes 3145732
  39.8 17.9 %all-to-all-start.1 = ((f32[16,128,128]{2,0,1:T(8,128)}), f32[16,128,128]{2,0,1:T(8,128)S(1)}, u32[]{:S(2)}, u32[]{:S(2)}) async-start(f32[16,128,128]{2,0,1:T(8,128)} %copy.27), calls=%async_computation.1 | async-start | bytes 2097152 | tf_op jit(solution)/shard_map/all_to_all | solution.py:33
  43.5 0.7 copy-start.2
  44.2 0.7 copy-start.3
  58.4 0.7 %copy-start.1 = (f32[512]{0:T(512)S(1)}, f32[512]{0:T(512)}, u32[]{:S(2)}) copy-start(f32[512]{0:T(512)} %param.7) | copy-start | bytes 6148
where the time goes:
time: 66.3 us; the launch traced here: 66 us
  blocking collectives  32.9 us (50%)
  waiting for transfers between devices  12.7 us (19%)
  matrix products  10.5 us (16%)
  local copies, waits for them, and re-layouts  6.11 us (9%)
  starting transfers between devices  3.7 us (6%)
    all_to_all x1, blocking collectives, per_device(): lax.all_to_all(part_values, 'row', split_axis=0, concat_axis=1, tiled=True)  32.9 us
    all_to_all x1, waiting for transfers between devices, per_device(): lax.all_to_all(local_values, 'col', split_axis=1, concat_axis=2, tiled=True)  12.7 us
    dot_general x3, matrix products, to_modes(): jnp.tensordot(values, transform_table(values.shape[dim]), axes=([dim], [0...  10.5 us
    all_to_all x1, starting transfers between devices, per_device(): lax.all_to_all(local_values, 'col', split_axis=1, concat_axis=2, tiled=True)  3.7 us
    unnamed x8, local copies, waits for them, and re-layouts  2.77 us
    transpose x1, local copies, waits for them, and re-layouts, to_modes(): return jnp.moveaxis(moved, -1, dim)  1.38 us
  transfers between devices with their start and end apart: 1, of which 1 were waited for; matrix products, arithmetic and copies ran while one was open for 0% of the time, Pallas kernels for 0%

commit v1 on v0

v1 whole, which is shorter than its diff:
```python
import functools

import jax
import jax.numpy as jnp
import numpy as np
from jax import lax
from jax.experimental import pallas as pl
from jax.experimental.pallas import tpu as pltpu
from jax.sharding import PartitionSpec as P

SPLIT = (8, 8)
GROUP = 4
F32, BF16 = jnp.float32, jnp.bfloat16
VMEM = pl.BlockSpec(memory_space=pltpu.VMEM)
HBM = pl.BlockSpec(memory_space=pltpu.HBM)


def table(count):
    rank = np.arange(1, count + 1, dtype=np.int64)
    angle = np.pi / (count + 1) * (rank[:, None] * rank[None, :] % (2 * count + 2))
    return (np.sin(angle) * (2.0 / (count + 1)) ** 0.5).astype(np.float32)


def halves(values):
    high = values.astype(BF16)
    return high, (values - high.astype(F32)).astype(BF16)


def product(left, right):
    lh, ll = left
    rh, rl = right
    dot = functools.partial(jnp.dot, preferred_element_type=F32)
    return dot(lh, rh) + (dot(ll, rh) + dot(lh, rl))


def call(kernel, outs, flops, ins, out_specs=None, scratch=(), vmem=24 * 2**20, **kw):
    return pl.pallas_call(
        kernel,
        out_shape=outs,
        in_specs=ins,
        out_specs=out_specs if out_specs is not None else [VMEM] * len(outs),
        scratch_shapes=list(scratch),
        compiler_params=pltpu.CompilerParams(vmem_limit_bytes=vmem),
        cost_estimate=pl.CostEstimate(flops=flops, bytes_accessed=0, transcendentals=0),
        **kw,
    )


def sines(left, right, count):
    turns = left.astype(F32) * right.astype(F32)
    period = 2 * count + 2
    turns = turns - jnp.floor(turns * (1.0 / period)) * period - (count + 1)
    return jnp.sin(turns * (-np.pi / (count + 1))) * np.float32((2.0 / (count + 1)) ** 0.5)


def prepare(rows, cols, xh, xl, yh, yl):
    r, c = lax.axis_index("row"), lax.axis_index("col")
    nx, ny = xh.shape[0], yh.shape[0]
    bx, by, bk = nx // rows, ny // rows, ny // cols

    def ramp(count, dim):
        return lax.broadcasted_iota(jnp.int32, (count, 1) if dim == 0 else (1, count), dim)

    across = ramp(nx, 1)
    for d in range(rows):
        at = slice(d * bx, (d + 1) * bx)
        xh[at], xl[at] = halves(sines(ramp(bx, 0) + ((r ^ d) * bx + 1), across + 1, nx))
    across = ramp(ny, 1)
    source = jnp.zeros_like(across)
    for d in range(rows):
        source = jnp.where((across >= d * by) & (across < (d + 1) * by), across + ((r ^ d) * by - d * by + 1), source)
    for e in range(cols):
        at = slice(e * bk, (e + 1) * bk)
        yh[at], yl[at] = halves(sines(ramp(bk, 0) + ((c ^ e) * bk + 1), source, ny))


def x_modes(plan, bx, t_ref, hh_ref, hl_ref, *outs):
    nx, by, bz = t_ref.shape
    left = hh_ref[...], hl_ref[...]
    flat_t = t_ref.reshape(nx * by, bz)
    flat_o = [o.reshape(int(np.prod(o.shape[:-1])), bz) for o in outs]
    for y in range(0, by, 2):
        right = jnp.concatenate([flat_t[pl.ds(y + i, nx, stride=by), :] for i in range(2)], axis=1)
        res = product(left, halves(right))
        for blocks, o in zip(plan, flat_o):
            base = 0
            for d, lo, s in blocks:
                for i in range(2):
                    o[pl.ds(base * by + y + i, s, stride=by), :] = res[d * bx + lo:d * bx + lo + s, i * bz:(i + 1) * bz]
                base += s


def join(keep, came, *outs):
    for h, o in enumerate(outs):
        o[0] = keep[h + 1]
        o[1] = came[h + 1]


def y_modes(places, cols, hh_ref, hl_ref, *refs):
    pieces, outs = refs[:-cols], refs[-cols:]
    s, bk, bz = outs[0].shape
    left = hh_ref[...], hl_ref[...]
    for k in range(0, s, 2):
        ks = range(k, min(k + 2, s))
        right = jnp.concatenate(
            [jnp.concatenate([pieces[i][q] if at is None else pieces[i][at, q] for i, at in places], axis=0) for q in ks], axis=1)
        res = product(left, halves(right))
        for i, q in enumerate(ks):
            for e in range(cols):
                outs[e][q] = res[e * bk:(e + 1) * bk, i * bz:(i + 1) * bz]


def z_part(hh_ref, hl_ref, pieces, es, k0, k1):
    c = lax.axis_index("col")
    _, bk, bz = pieces[0].shape
    left = jnp.concatenate([p[k0:k1].reshape((k1 - k0) * bk, bz) for p in pieces], axis=1)
    ats = [pl.ds(pl.multiple_of((c ^ e) * bz, bz), bz) for e in es]
    right = tuple(jnp.concatenate([h[at, :] for at in ats], axis=0) for h in (hh_ref, hl_ref))
    return product(halves(left), right)


def z_first(lo, half, hh_ref, hl_ref, sx_ref, sy_ref, sz_ref, *refs):
    pieces, (acc, fac, scr_x, scr_y) = refs[:half], refs[half:]
    s, bk, nz = acc.shape
    bx = sx_ref.shape[1] // lax.axis_size("row")
    r, c = lax.axis_index("row"), lax.axis_index("col")
    nx, ny = sx_ref.shape[1], sy_ref.shape[1]
    scr_x[...] = jnp.broadcast_to(sx_ref[...], (128, nx)).T
    scr_y[...] = jnp.broadcast_to(sy_ref[...], (128, ny)).T
    col = scr_y[pl.ds(pl.multiple_of(c * bk, bk), bk), :]
    for k in range(s):
        base = col + scr_x[pl.ds(r * bx + lo + k, 1), :]
        sym = 0.2 * (jnp.concatenate([base] * (nz // 128), axis=1) + sz_ref[...])
        fac[k] = (1.0 - sym) / (1.0 + sym)
    acc[...] = z_part(hh_ref, hl_ref, pieces, list(range(half)), 0, s).reshape(s, bk, nz)


def z_last(lo, half, group, hh_ref, hl_ref, acc, fac, *refs):
    pieces, (out, buf, sems) = refs[:half], refs[-3:]
    s, bk, nz = acc.shape
    copies = []
    for i, k in enumerate(range(0, s, group)):
        e = min(k + group, s)
        part = z_part(hh_ref, hl_ref, pieces, list(range(half, 2 * half)), k, e).reshape(e - k, bk, nz)
        buf[k:e] = (acc[k:e] + part) * fac[k:e]
        copies.append(pltpu.make_async_copy(buf.at[pl.ds(k, e - k)], out.at[pl.ds(lo + k, e - k)], sems.at[i]))
        copies[-1].start()
    for copy in copies:
        copy.wait()


def make(rows, cols):
    def shape(*dims):
        return jax.ShapeDtypeStruct(dims, F32)

    def per_device(tracer, symbol_x, symbol_y, symbol_z):
        nx, by, bz = tracer.shape
        ny, nz = by * rows, bz * cols
        bx, bk = nx // rows, ny // cols
        half = cols // 2
        far, near = range(rows // 2, rows), range(1, rows // 2)
        sizes = [w * bx // 16 for w in SPLIT]
        starts = [sum(sizes[:j]) for j in range(len(sizes))]
        chunks = list(zip(starts, sizes))
        hz = table(nz)
        hzh = hz.astype(jnp.bfloat16)
        hzl = jnp.asarray((hz - hzh.astype(np.float32)).astype(jnp.bfloat16))
        hzh = jnp.asarray(hzh)

        def send(value, axis, d, n):
            return lax.ppermute(value, axis, [(i, i ^ d) for i in range(n)])

        xh, xl, yh, yl = call(
            functools.partial(prepare, rows, cols), [jax.ShapeDtypeStruct((n, n), BF16) for n in (nx, nx, ny, ny)],
            10**9, [])()
        (l0, s0), (l1, s1) = chunks
        deep = rows // 2
        plan = [[(d, l0, s0)] for d in range(rows)]
        plan += [[(2 * h + 1, l1, s1) for h in range(deep)], [(2 * h, l1, s1) for h in range(deep)]]
        u = call(
            functools.partial(x_modes, plan, bx), [shape(s0, by, bz)] * rows + [shape(deep, s1, by, bz)] * 2, 10**8, [VMEM] * 3,
        )(tracer, xh, xl)
        got = {0: u[0]}
        for d in far:
            got[d] = send(u[d], "row", d, rows)
        for d in near:
            got[d] = send(u[d], "row", d, rows)
        keep = u[-1]
        came = send(u[-2], "row", 1, rows)
        both = call(join, [shape(2, s1, by, bz)] * (deep - 1), 10**6, [VMEM] * 2)(keep, came)
        full = [send(both[h - 1], "row", 2 * h, rows) for h in range(1, deep)]

        sx, sy, sz = symbol_x.reshape(1, nx), symbol_y.reshape(1, ny), symbol_z.reshape(1, nz)
        out = None
        for j, (lo, s) in enumerate(chunks):
            if j == 0:
                pieces = [got[d] for d in range(rows)]
                places = [(d, None) for d in range(rows)]
            else:
                pieces = [keep, came] + full
                places = [(0, 0), (1, 0)] + [(2 + h, i) for h in range(deep - 1) for i in range(2)]
            w = call(
                functools.partial(y_modes, places, cols), [shape(s, bk, bz)] * cols,
                10**8, [VMEM] * (2 + len(pieces)))(yh, yl, *pieces)
            w = list(w)
            for e in list(range(half, cols)) + list(range(1, half)):
                w[e] = send(w[e], "col", e, cols)
            acc, fac = call(
                functools.partial(z_first, lo, half), [shape(s, bk, nz)] * 2, 10**8,
                [VMEM] * (5 + half), scratch=[pltpu.VMEM((nx, 128), F32), pltpu.VMEM((ny, 128), F32)],
            )(hzh, hzl, sx, sy, sz, *w[:half])
            prev = [] if out is None else [out]
            out = call(
                functools.partial(z_last, lo, half, GROUP), shape(bx, bk, nz), 10**8,
                [VMEM] * (4 + half) + [HBM] * len(prev), out_specs=HBM,
                scratch=[pltpu.VMEM((s, bk, nz), F32), pltpu.SemaphoreType.DMA((-(-s // GROUP),))],
                input_output_aliases={4 + half: 0} if prev else {},
            )(hzh, hzl, acc, fac, *w[half:], *prev)
        return out

    return per_device


def solution(mesh):
    rows, cols = mesh.shape["row"], mesh.shape["col"]


    body = make(rows, cols)

    in_specs = (P(None, "row", "col"), P(), P(), P())
    return jax.shard_map(body, mesh=mesh, in_specs=in_specs, out_specs=P("row", "col", None), check_vma=False)
```

time: 66.3 us -> 43.4 us (0.65)
  blocking collectives: 32.9 us -> 0 us
  starting transfers between devices: 3.7 us -> 20.9 us
  matrix products: 10.5 us -> 0 us
  Pallas kernels: 0 us -> 5.02 us
  local copies, waits for them, and re-layouts: 6.11 us -> 1.41 us
  waiting for transfers between devices: 12.7 us -> 15.8 us
    all_to_all x1 -> x0, blocking collectives: 32.9 us -> none  [per_device(): lax.all_to_all(part_values, 'row', split_axis=0, concat_axis=1, tiled=True)]
    ppermute x0 -> x17, starting transfers between devices: none -> 20.9 us  [send(): return lax.ppermute(value, axis, [(i, i ^ d) for i in range(n)])]
    ppermute x0 -> x17, waiting for transfers between devices: none -> 15.8 us  [send(): return lax.ppermute(value, axis, [(i, i ^ d) for i in range(n)])]
    all_to_all x1 -> x0, waiting for transfers between devices: 12.7 us -> none  [per_device(): lax.all_to_all(local_values, 'col', split_axis=1, concat_axis=2, tiled=True)]
    dot_general x3 -> x0, matrix products: 10.5 us -> none  [to_modes(): jnp.tensordot(values, transform_table(values.shape[dim]), axes=([dim], [0...]
    pallas_call x0 -> x9, Pallas kernels: none -> 5.02 us  [the longest x2 2.23 us: per_device(): call(functools.partial(z_last, lo, half, GROUP), shape(bx, bk, nz), 10 **...]
    all_to_all x1 -> x0, starting transfers between devices: 3.7 us -> none  [per_device(): lax.all_to_all(local_values, 'col', split_axis=1, concat_axis=2, tiled=True)]
    transpose x1 -> x0, local copies, waits for them, and re-layouts: 1.38 us -> none  [to_modes(): return jnp.moveaxis(moved, -1, dim)]
  transfers between devices with their start and end apart: 1 -> 17, of which waited for: 1 -> 6; matrix products, arithmetic and copies ran while one was open for 0% -> 0% of each run, Pallas kernels for 0% -> 6%
where the time goes in v1:
time: 43.4 us; the launch traced here: 43.3 us
  starting transfers between devices  20.9 us (48%)
  waiting for transfers between devices  15.8 us (36%)
  Pallas kernels  5.02 us (12%)
  local copies, waits for them, and re-layouts  1.41 us (3%)
    ppermute x17, starting transfers between devices, send(): return lax.ppermute(value, axis, [(i, i ^ d) for i in range(n)])  20.9 us
    ppermute x17, waiting for transfers between devices, send(): return lax.ppermute(value, axis, [(i, i ^ d) for i in range(n)])  15.8 us
    pallas_call x2, Pallas kernels, per_device(): call(functools.partial(z_last, lo, half, GROUP), shape(bx, bk, nz), 10 **...  2.23 us
    unnamed x12, local copies, waits for them, and re-layouts  1.41 us
  transfers between devices with their start and end apart: 17, of which 6 were waited for; matrix products, arithmetic and copies ran while one was open for 0% of the time, Pallas kernels for 6%

profile of v1, /device:TPU:0, one launch (start us, length us, event | category | flops | bytes accessed | tf_op | source)
XLA Modules:
  0.0 43.3 jit_solution(4682998821583094522)
XLA Ops:
  0.0 0.5 %shard_map.64 = (bf16[128,128]{1,0:T(8,128)(2,1)S(1)}, bf16[128,128]{1,0:T(8,128)(2,1)S(1)}, bf16[128,128]{1,0:T(8,128)(2,1)S(1)}, bf16[128,128]{1,0:T(8,128)(2,1)S(1)}) custom-call(), custom_call_target="tpu_custom_call" | custom-call | flops 1000000000 | tf_op jit(solution)/shard_map/pallas_call | solution.py:173
  0.5 0.7 %copy-done.2 = f32[128,16,128]{2,1,0:T(8,128)S(1)} copy-done((f32[128,16,128]{2,1,0:T(8,128)S(1)}, f32[128,16,128]{2,1,0:T(8,128)}, u32[]{:S(2)}) %copy-start.2) | copy-done | bytes 1048600
  1.2 0.8 %shard_map.65 = (f32[8,16,128]{2,1,0:T(8,128)S(1)}, f32[8,16,128]{2,1,0:T(8,128)S(1)}, f32[8,16,128]{2,1,0:T(8,128)S(1)}, f32[8,16,128]{2,1,0:T(8,128)S(1)}, f32...) custom-call(f32[128,16,128]{2,1,0:T(8,128)S(1)} %copy-done.2, ...), custom_call_target="tpu_custom_call" | custom-call | flops 100000000 | tf_op jit(solution)/shard_map/pallas_call | solution.py:180
  2.0 3.1 %collective-permute-start = (f32[4,8,16,128]{3,2,1,0:T(8,128)S(1)}, f32[4,8,16,128]{3,2,1,0:T(8,128)S(1)}, u32[]{:S(2)}, u32[]{:S(2)}) collective-permute-start(f32[4,8,16,128]{3,2,1,0:T(8,128)S(1)} %get-tuple-element.39), channel_id=1, source_target_pairs={{0,4},{4,0},{8,12},{12,8},{16,20},{20,16},{24,28},{28,24},{1,5},{5... | collective-permute-start | bytes 786440 | tf_op jit(solution)/shard_map/ppermute | solution.py:171
  5.1 2.6 %collective-permute-start.10 = (f32[8,16,128]{2,1,0:T(8,128)S(1)}, f32[8,16,128]{2,1,0:T(8,128)S(1)}, u32[]{:S(2)}, u32[]{:S(2)}) collective-permute-start(f32[8,16,128]{2,1,0:T(8,128)S(1)} %get-tuple-element.53), channel_id=1, source_target_pairs={{0,16},{4,20},{8,24},{12,28},{16,0},{20,4},{24,8},{28,12},{1,17},{... | collective-permute-start | bytes 196616 | tf_op jit(solution)/shard_map/ppermute | solution.py:171
  7.7 0.0 collective-permute-start.11
  7.7 3.9 %collective-permute-start.12 = (f32[8,16,128]{2,1,0:T(8,128)S(1)}, f32[8,16,128]{2,1,0:T(8,128)S(1)}, u32[]{:S(2)}, u32[]{:S(2)}) collective-permute-start(f32[8,16,128]{2,1,0:T(8,128)S(1)} %get-tuple-element.55), channel_id=1, source_target_pairs={{0,24},{4,28},{8,16},{12,20},{16,8},{20,12},{24,0},{28,4},{1,25},{... | collective-permute-start | bytes 196616 | tf_op jit(solution)/shard_map/ppermute | solution.py:171
  11.5 1.2 %collective-permute-start.13 = (f32[8,16,128]{2,1,0:T(8,128)S(1)}, f32[8,16,128]{2,1,0:T(8,128)S(1)}, u32[]{:S(2)}, u32[]{:S(2)}) collective-permute-start(f32[8,16,128]{2,1,0:T(8,128)S(1)} %get-tuple-element.56), channel_id=1, source_target_pairs={{0,28},{4,24},{8,20},{12,16},{16,12},{20,8},{24,4},{28,0},{1,29},{... | collective-permute-start | bytes 196616 | tf_op jit(solution)/shard_map/ppermute | solution.py:171
  12.7 0.1 collective-permute-done.10.refs_4_
  12.8 0.3 collective-permute-start.7
  13.1 4.3 %collective-permute-done.11.refs_5_ = f32[8,16,128]{2,1,0:T(8,128)S(1)} collective-permute-done((f32[8,16,128]{2,1,0:T(8,128)S(1)}, f32[8,16,128]{2,1,0:T(8,128)S(1)}, u32[]{:S(2)}, u32[]{:S(2)}) %collective-permute-start.11) | collective-permute-done | bytes 65568 | tf_op jit(solution)/shard_map/ppermute | solution.py:171
  17.3 0.0 collective-permute-start.8
  17.3 0.0 collective-permute-done.came.refs_1_
  17.4 1.2 %collective-permute-start.9 = (f32[8,16,128]{2,1,0:T(8,128)S(1)}, f32[8,16,128]{2,1,0:T(8,128)S(1)}, u32[]{:S(2)}, u32[]{:S(2)}) collective-permute-start(f32[8,16,128]{2,1,0:T(8,128)S(1)} %get-tuple-element.52), channel_id=1, source_target_pairs={{0,12},{4,8},{8,4},{12,0},{16,28},{20,24},{24,20},{28,16},{1,13},{... | collective-permute-start | bytes 196616 | tf_op jit(solution)/shard_map/ppermute | solution.py:171
  18.6 0.0 collective-permute-done.12.refs_6_
  18.6 1.0 %collective-permute-start.1 = (f32[2,8,16,128]{3,2,1,0:T(8,128)S(1)}, f32[2,8,16,128]{3,2,1,0:T(8,128)S(1)}, u32[]{:S(2)}, u32[]{:S(2)}) collective-permute-start(f32[2,8,16,128]{3,2,1,0:T(8,128)S(1)} %get-tuple-element.40), channel_id=1, source_target_pairs={{0,8},{4,12},{8,0},{12,4},{16,24},{20,28},{24,16},{28,20},{1,9},{5... | collective-permute-start | bytes 393224 | tf_op jit(solution)/shard_map/ppermute | solution.py:171
  19.6 0.0 collective-permute-done.13.refs_7_
  19.6 4.1 %collective-permute-start.2 = (f32[2,8,16,128]{3,2,1,0:T(8,128)S(1)}, f32[2,8,16,128]{3,2,1,0:T(8,128)S(1)}, u32[]{:S(2)}, u32[]{:S(2)}) collective-permute-start(f32[2,8,16,128]{3,2,1,0:T(8,128)S(1)} %get-tuple-element.41), channel_id=1, source_target_pairs={{0,16},{4,20},{8,24},{12,28},{16,0},{20,4},{24,8},{28,12},{1,17},{... | collective-permute-start | bytes 393224 | tf_op jit(solution)/shard_map/ppermute | solution.py:171
  23.7 0.0 collective-permute-done.7.refs_1_
  23.7 0.0 collective-permute-start.3
  23.7 0.0 collective-permute-done.8.refs_2_
  23.7 0.0 collective-permute-done.9.refs_3_
  23.7 0.0 copy-start.1
  23.8 0.4 shard_map.69
  24.1 0.0 copy-start
  24.1 0.1 collective-permute-start.14
  24.2 1.6 %collective-permute-start.15 = (f32[8,32,128]{2,1,0:T(8,128)S(1)}, f32[8,32,128]{2,1,0:T(8,128)S(1)}, u32[]{:S(2)}, u32[]{:S(2)}) collective-permute-start(f32[8,32,128]{2,1,0:T(8,128)S(1)} %get-tuple-element.61), channel_id=1, source_target_pairs={{0,2},{1,3},{2,0},{3,1},{4,6},{5,7},{6,4},{7,5},{8,10},{9,11},{10,... | collective-permute-start | bytes 393224 | tf_op jit(solution)/shard_map/ppermute | solution.py:171
  25.8 0.9 %collective-permute-done.1.refs_2_ = f32[2,8,16,128]{3,2,1,0:T(8,128)S(1)} collective-permute-done((f32[2,8,16,128]{3,2,1,0:T(8,128)S(1)}, f32[2,8,16,128]{3,2,1,0:T(8,128)S(1)}, u32[]{:S(2)}, u32[]{:S(2)}) %collective-permute-start.1) | collective-permute-done | bytes 131104 | tf_op jit(solution)/shard_map/ppermute | solution.py:171
  26.6 0.0 collective-permute-start.16
  26.6 6.9 %collective-permute-done.2.refs_3_ = f32[2,8,16,128]{3,2,1,0:T(8,128)S(1)} collective-permute-done((f32[2,8,16,128]{3,2,1,0:T(8,128)S(1)}, f32[2,8,16,128]{3,2,1,0:T(8,128)S(1)}, u32[]{:S(2)}, u32[]{:S(2)}) %collective-permute-start.2) | collective-permute-done | bytes 131104 | tf_op jit(solution)/shard_map/ppermute | solution.py:171
  33.5 0.0 collective-permute-done.3.refs_4_
  33.5 0.4 shard_map.67
  33.9 0.1 collective-permute-start.4
  34.0 1.6 %collective-permute-start.5 = (f32[8,32,128]{2,1,0:T(8,128)S(1)}, f32[8,32,128]{2,1,0:T(8,128)S(1)}, u32[]{:S(2)}, u32[]{:S(2)}) collective-permute-start(f32[8,32,128]{2,1,0:T(8,128)S(1)} %get-tuple-element.47), channel_id=1, source_target_pairs={{0,2},{1,3},{2,0},{3,1},{4,6},{5,7},{6,4},{7,5},{8,10},{9,11},{10,... | collective-permute-start | bytes 393224 | tf_op jit(solution)/shard_map/ppermute | solution.py:171
  35.5 0.0 collective-permute-done.14.refs_1_
  35.5 0.3 collective-permute-start.6
  35.8 0.0 copy-done.1
  35.9 0.0 copy-done
  35.9 0.7 %copy-done.3 = f32[512]{0:T(512)S(1)} copy-done((f32[512]{0:T(512)S(1)}, f32[512]{0:T(512)}, u32[]{:S(2)}) %copy-start.3) | copy-done | bytes 2072
  36.5 0.4 shard_map.70
  36.9 0.0 collective-permute-done.15.refs_0_
  36.9 0.0 collective-permute-done.16.refs_1_
  36.9 1.1 %shard_map.71.refs_2_ = f32[16,32,512]{2,1,0:T(8,128)} custom-call(bf16[512,512]{1,0:T(8,128)(2,1)S(1)} %copy-done.1, bf16[512,512]{1,0:T(8,128)(2,1)S(1)} %copy-done, f32[8,32,512]{2,1,0:T(8,128)S(1)} %get-tuple-element.59.acc, f32[8,32,512]{2,1,0:T(8,128)S(1)} %get-tuple-element.60.fac, f32[8,32,128]{2,1,0:T(8,128)S(1)} %collective-permute-done.15.refs_0_, ...), custom_call_target="tpu_custom_call" | custom-call | flops 100000000 | tf_op jit(solution)/shard_map/pallas_call | solution.py:213
  38.1 0.0 collective-permute-done.4.refs_1_
  38.1 0.4 shard_map.68
  38.5 2.0 %collective-permute-done.5.refs_0_ = f32[8,32,128]{2,1,0:T(8,128)S(1)} collective-permute-done((f32[8,32,128]{2,1,0:T(8,128)S(1)}, f32[8,32,128]{2,1,0:T(8,128)S(1)}, u32[]{:S(2)}, u32[]{:S(2)}) %collective-permute-start.5) | collective-permute-done | bytes 131104 | tf_op jit(solution)/shard_map/ppermute | solution.py:171
  40.4 1.7 %collective-permute-done.6.refs_1_ = f32[8,32,128]{2,1,0:T(8,128)S(1)} collective-permute-done((f32[8,32,128]{2,1,0:T(8,128)S(1)}, f32[8,32,128]{2,1,0:T(8,128)S(1)}, u32[]{:S(2)}, u32[]{:S(2)}) %collective-permute-start.6) | collective-permute-done | bytes 131104 | tf_op jit(solution)/shard_map/ppermute | solution.py:171
  42.2 1.1 %shard_map.72 = f32[16,32,512]{2,1,0:T(8,128)} custom-call(bf16[512,512]{1,0:T(8,128)(2,1)S(1)} %copy-done.1, bf16[512,512]{1,0:T(8,128)(2,1)S(1)} %copy-done, f32[8,32,512]{2,1,0:T(8,128)S(1)} %get-tuple-element.45.acc, f32[8,32,512]{2,1,0:T(8,128)S(1)} %get-tuple-element.46.fac, ...), custom_call_target="tpu_custom_call", output_to_operand_aliasing={{}: (6, {})} | custom-call | flops 100000000 | tf_op jit(solution)/shard_map/pallas_call | solution.py:213
  (7 shorter events, 0.0 us)
Async XLA Ops:
  0.0 1.2 %copy-start.2 = (f32[128,16,128]{2,1,0:T(8,128)S(1)}, f32[128,16,128]{2,1,0:T(8,128)}, u32[]{:S(2)}) copy-start(f32[128,16,128]{2,1,0:T(8,128)} %t_ref.1) | copy-start | bytes 3145732
  2.0 15.3 %collective-permute-start = (f32[4,8,16,128]{3,2,1,0:T(8,128)S(1)}, f32[4,8,16,128]{3,2,1,0:T(8,128)S(1)}, u32[]{:S(2)}, u32[]{:S(2)}) collective-permute-start(f32[4,8,16,128]{3,2,1,0:T(8,128)S(1)} %get-tuple-element.39), channel_id=1, source_target_pairs={{0,4},{4,0},{8,12},{12,8},{16,20},{20,16},{24,28},{28,24},{1,5},{5... | collective-permute-start | bytes 786440 | tf_op jit(solution)/shard_map/ppermute | solution.py:171
  5.1 7.7 %collective-permute-start.10 = (f32[8,16,128]{2,1,0:T(8,128)S(1)}, f32[8,16,128]{2,1,0:T(8,128)S(1)}, u32[]{:S(2)}, u32[]{:S(2)}) collective-permute-start(f32[8,16,128]{2,1,0:T(8,128)S(1)} %get-tuple-element.53), channel_id=1, source_target_pairs={{0,16},{4,20},{8,24},{12,28},{16,0},{20,4},{24,8},{28,12},{1,17},{... | collective-permute-start | bytes 196616 | tf_op jit(solution)/shard_map/ppermute | solution.py:171
  7.7 9.7 %collective-permute-start.11 = (f32[8,16,128]{2,1,0:T(8,128)S(1)}, f32[8,16,128]{2,1,0:T(8,128)S(1)}, u32[]{:S(2)}, u32[]{:S(2)}) collective-permute-start(f32[8,16,128]{2,1,0:T(8,128)S(1)} %get-tuple-element.54), channel_id=1, source_target_pairs={{0,20},{4,16},{8,28},{12,24},{16,4},{20,0},{24,12},{28,8},{1,21},{... | collective-permute-start | bytes 196616 | tf_op jit(solution)/shard_map/ppermute | solution.py:171
  7.7 10.9 %collective-permute-start.12 = (f32[8,16,128]{2,1,0:T(8,128)S(1)}, f32[8,16,128]{2,1,0:T(8,128)S(1)}, u32[]{:S(2)}, u32[]{:S(2)}) collective-permute-start(f32[8,16,128]{2,1,0:T(8,128)S(1)} %get-tuple-element.55), channel_id=1, source_target_pairs={{0,24},{4,28},{8,16},{12,20},{16,8},{20,12},{24,0},{28,4},{1,25},{... | collective-permute-start | bytes 196616 | tf_op jit(solution)/shard_map/ppermute | solution.py:171
  11.5 8.1 %collective-permute-start.13 = (f32[8,16,128]{2,1,0:T(8,128)S(1)}, f32[8,16,128]{2,1,0:T(8,128)S(1)}, u32[]{:S(2)}, u32[]{:S(2)}) collective-permute-start(f32[8,16,128]{2,1,0:T(8,128)S(1)} %get-tuple-element.56), channel_id=1, source_target_pairs={{0,28},{4,24},{8,20},{12,16},{16,12},{20,8},{24,4},{28,0},{1,29},{... | collective-permute-start | bytes 196616 | tf_op jit(solution)/shard_map/ppermute | solution.py:171
  12.8 10.9 %collective-permute-start.7 = (f32[8,16,128]{2,1,0:T(8,128)S(1)}, f32[8,16,128]{2,1,0:T(8,128)S(1)}, u32[]{:S(2)}, u32[]{:S(2)}) collective-permute-start(f32[8,16,128]{2,1,0:T(8,128)S(1)} %get-tuple-element.50), channel_id=1, source_target_pairs={{0,4},{4,0},{8,12},{12,8},{16,20},{20,16},{24,28},{28,24},{1,5},{5... | collective-permute-start | bytes 196616 | tf_op jit(solution)/shard_map/ppermute | solution.py:171
  17.3 6.4 %collective-permute-start.8 = (f32[8,16,128]{2,1,0:T(8,128)S(1)}, f32[8,16,128]{2,1,0:T(8,128)S(1)}, u32[]{:S(2)}, u32[]{:S(2)}) collective-permute-start(f32[8,16,128]{2,1,0:T(8,128)S(1)} %get-tuple-element.51), channel_id=1, source_target_pairs={{0,8},{4,12},{8,0},{12,4},{16,24},{20,28},{24,16},{28,20},{1,9},{5... | collective-permute-start | bytes 196616 | tf_op jit(solution)/shard_map/ppermute | solution.py:171
  17.4 6.4 %collective-permute-start.9 = (f32[8,16,128]{2,1,0:T(8,128)S(1)}, f32[8,16,128]{2,1,0:T(8,128)S(1)}, u32[]{:S(2)}, u32[]{:S(2)}) collective-permute-start(f32[8,16,128]{2,1,0:T(8,128)S(1)} %get-tuple-element.52), channel_id=1, source_target_pairs={{0,12},{4,8},{8,4},{12,0},{16,28},{20,24},{24,20},{28,16},{1,13},{... | collective-permute-start | bytes 196616 | tf_op jit(solution)/shard_map/ppermute | solution.py:171
  18.6 8.1 %collective-permute-start.1 = (f32[2,8,16,128]{3,2,1,0:T(8,128)S(1)}, f32[2,8,16,128]{3,2,1,0:T(8,128)S(1)}, u32[]{:S(2)}, u32[]{:S(2)}) collective-permute-start(f32[2,8,16,128]{3,2,1,0:T(8,128)S(1)} %get-tuple-element.40), channel_id=1, source_target_pairs={{0,8},{4,12},{8,0},{12,4},{16,24},{20,28},{24,16},{28,20},{1,9},{5... | collective-permute-start | bytes 393224 | tf_op jit(solution)/shard_map/ppermute | solution.py:171
  19.6 13.9 %collective-permute-start.2 = (f32[2,8,16,128]{3,2,1,0:T(8,128)S(1)}, f32[2,8,16,128]{3,2,1,0:T(8,128)S(1)}, u32[]{:S(2)}, u32[]{:S(2)}) collective-permute-start(f32[2,8,16,128]{3,2,1,0:T(8,128)S(1)} %get-tuple-element.41), channel_id=1, source_target_pairs={{0,16},{4,20},{8,24},{12,28},{16,0},{20,4},{24,8},{28,12},{1,17},{... | collective-permute-start | bytes 393224 | tf_op jit(solution)/shard_map/ppermute | solution.py:171
  23.7 9.8 %collective-permute-start.3 = (f32[2,8,16,128]{3,2,1,0:T(8,128)S(1)}, f32[2,8,16,128]{3,2,1,0:T(8,128)S(1)}, u32[]{:S(2)}, u32[]{:S(2)}) collective-permute-start(f32[2,8,16,128]{3,2,1,0:T(8,128)S(1)} %get-tuple-element.42), channel_id=1, source_target_pairs={{0,24},{4,28},{8,16},{12,20},{16,8},{20,12},{24,0},{28,4},{1,25},{... | collective-permute-start | bytes 393224 | tf_op jit(solution)/shard_map/ppermute | solution.py:171
  23.7 12.1 %copy-start.1 = (bf16[512,512]{1,0:T(8,128)(2,1)S(1)}, bf16[512,512]{1,0:T(8,128)(2,1)}, u32[]{:S(2)}) copy-start(bf16[512,512]{1,0:T(8,128)(2,1)} %constant.5.clone.hh_ref) | copy-start | bytes 1572868
  24.1 11.7 %copy-start = (bf16[512,512]{1,0:T(8,128)(2,1)S(1)}, bf16[512,512]{1,0:T(8,128)(2,1)}, u32[]{:S(2)}) copy-start(bf16[512,512]{1,0:T(8,128)(2,1)} %constant.4.clone.hl_ref) | copy-start | bytes 1572868
  24.1 11.4 %collective-permute-start.14 = (f32[8,32,128]{2,1,0:T(8,128)S(1)}, f32[8,32,128]{2,1,0:T(8,128)S(1)}, u32[]{:S(2)}, u32[]{:S(2)}) collective-permute-start(f32[8,32,128]{2,1,0:T(8,128)S(1)} %get-tuple-element.58), channel_id=1, source_target_pairs={{0,1},{1,0},{2,3},{3,2},{4,5},{5,4},{6,7},{7,6},{8,9},{9,8},{10,11... | collective-permute-start | bytes 393224 | tf_op jit(solution)/shard_map/ppermute | solution.py:171
  24.2 12.7 %collective-permute-start.15 = (f32[8,32,128]{2,1,0:T(8,128)S(1)}, f32[8,32,128]{2,1,0:T(8,128)S(1)}, u32[]{:S(2)}, u32[]{:S(2)}) collective-permute-start(f32[8,32,128]{2,1,0:T(8,128)S(1)} %get-tuple-element.61), channel_id=1, source_target_pairs={{0,2},{1,3},{2,0},{3,1},{4,6},{5,7},{6,4},{7,5},{8,10},{9,11},{10,... | collective-permute-start | bytes 393224 | tf_op jit(solution)/shard_map/ppermute | solution.py:171
  26.6 10.3 %collective-permute-start.16 = (f32[8,32,128]{2,1,0:T(8,128)S(1)}, f32[8,32,128]{2,1,0:T(8,128)S(1)}, u32[]{:S(2)}, u32[]{:S(2)}) collective-permute-start(f32[8,32,128]{2,1,0:T(8,128)S(1)} %get-tuple-element.62), channel_id=1, source_target_pairs={{0,3},{1,2},{2,1},{3,0},{4,7},{5,6},{6,5},{7,4},{8,11},{9,10},{10,... | collective-permute-start | bytes 393224 | tf_op jit(solution)/shard_map/ppermute | solution.py:171
  33.9 4.2 %collective-permute-start.4 = (f32[8,32,128]{2,1,0:T(8,128)S(1)}, f32[8,32,128]{2,1,0:T(8,128)S(1)}, u32[]{:S(2)}, u32[]{:S(2)}) collective-permute-start(f32[8,32,128]{2,1,0:T(8,128)S(1)} %get-tuple-element.44), channel_id=1, source_target_pairs={{0,1},{1,0},{2,3},{3,2},{4,5},{5,4},{6,7},{7,6},{8,9},{9,8},{10,11... | collective-permute-start | bytes 393224 | tf_op jit(solution)/shard_map/ppermute | solution.py:171
  34.0 6.4 %collective-permute-start.5 = (f32[8,32,128]{2,1,0:T(8,128)S(1)}, f32[8,32,128]{2,1,0:T(8,128)S(1)}, u32[]{:S(2)}, u32[]{:S(2)}) collective-permute-start(f32[8,32,128]{2,1,0:T(8,128)S(1)} %get-tuple-element.47), channel_id=1, source_target_pairs={{0,2},{1,3},{2,0},{3,1},{4,6},{5,7},{6,4},{7,5},{8,10},{9,11},{10,... | collective-permute-start | bytes 393224 | tf_op jit(solution)/shard_map/ppermute | solution.py:171
  35.5 6.6 %collective-permute-start.6 = (f32[8,32,128]{2,1,0:T(8,128)S(1)}, f32[8,32,128]{2,1,0:T(8,128)S(1)}, u32[]{:S(2)}, u32[]{:S(2)}) collective-permute-start(f32[8,32,128]{2,1,0:T(8,128)S(1)} %get-tuple-element.48), channel_id=1, source_target_pairs={{0,3},{1,2},{2,1},{3,0},{4,7},{5,6},{6,5},{7,4},{8,11},{9,10},{10,... | collective-permute-start | bytes 393224 | tf_op jit(solution)/shard_map/ppermute | solution.py:171
  35.8 0.7 %copy-start.3 = (f32[512]{0:T(512)S(1)}, f32[512]{0:T(512)}, u32[]{:S(2)}) copy-start(f32[512]{0:T(512)} %param.9) | copy-start | bytes 6148
  35.8 0.7 %copy-start.4 = (f32[128]{0:T(128)S(1)}, f32[128]{0:T(128)}, u32[]{:S(2)}) copy-start(f32[128]{0:T(128)} %param.7) | copy-start | bytes 1540
  35.8 0.7 %copy-start.5 = (f32[128]{0:T(128)S(1)}, f32[128]{0:T(128)}, u32[]{:S(2)}) copy-start(f32[128]{0:T(128)} %param.8) | copy-start | bytes 1540

commit v2 on v1

--- a/solution.py
+++ b/solution.py
@@ -8,7 +8,7 @@
 from jax.experimental.pallas import tpu as pltpu
 from jax.sharding import PartitionSpec as P
 
-SPLIT = (8, 8)
+SPLIT = (9, 7)
 GROUP = 4
 F32, BF16 = jnp.float32, jnp.bfloat16
 VMEM = pl.BlockSpec(memory_space=pltpu.VMEM)
@@ -30,7 +30,11 @@
     lh, ll = left
     rh, rl = right
     dot = functools.partial(jnp.dot, preferred_element_type=F32)
-    return dot(lh, rh) + (dot(ll, rh) + dot(lh, rl))
+    if lh.shape[1] <= 128:
+        return dot(jnp.concatenate([lh, ll], axis=1), jnp.concatenate([rh, rh], axis=0)) + dot(lh, rl)
+    m = lh.shape[0]
+    both = dot(jnp.concatenate([lh, ll], axis=0), rh)
+    return both[:m] + (both[m:] + dot(lh, rl))
 
 
 def call(kernel, outs, flops, ins, out_specs=None, scratch=(), vmem=24 * 2**20, **kw):

time: 43.4 us -> 47.5 us (1.094)
  the two profiles are of different devices: /device:TPU:0 before, /device:TPU:17 now
where the time goes in v2:
time: 47.5 us; the launch traced here: 47.4 us
  starting transfers between devices  24.3 us (51%)
  waiting for transfers between devices  16.7 us (35%)
  Pallas kernels  4.81 us (10%)
  local copies, waits for them, and re-layouts  1.4 us (3%)
    ppermute x17, starting transfers between devices, send(): return lax.ppermute(value, axis, [(i, i ^ d) for i in range(n)])  24.3 us
    ppermute x17, waiting for transfers between devices, send(): return lax.ppermute(value, axis, [(i, i ^ d) for i in range(n)])  16.7 us
    pallas_call x2, Pallas kernels, per_device(): call(functools.partial(z_last, lo, half, GROUP), shape(bx, bk, nz), 10 **...  2.19 us
    unnamed x12, local copies, waits for them, and re-layouts  1.4 us
  transfers between devices with their start and end apart: 17, of which 6 were waited for; matrix products, arithmetic and copies ran while one was open for 0% of the time, Pallas kernels for 5%

profile of v2, /device:TPU:17, one launch (start us, length us, event | category | flops | bytes accessed | tf_op | source)
XLA Modules:
  0.0 47.4 jit_solution(3103895257182889028)
XLA Ops:
  0.0 0.5 %shard_map.64 = (bf16[128,128]{1,0:T(8,128)(2,1)S(1)}, bf16[128,128]{1,0:T(8,128)(2,1)S(1)}, bf16[128,128]{1,0:T(8,128)(2,1)S(1)}, bf16[128,128]{1,0:T(8,128)(2,1)S(1)}) custom-call(), custom_call_target="tpu_custom_call" | custom-call | flops 1000000000 | tf_op jit(solution)/shard_map/pallas_call | solution.py:177
  0.5 0.7 %copy-done.2 = f32[128,16,128]{2,1,0:T(8,128)S(1)} copy-done((f32[128,16,128]{2,1,0:T(8,128)S(1)}, f32[128,16,128]{2,1,0:T(8,128)}, u32[]{:S(2)}) %copy-start.2) | copy-done | bytes 1048600
  1.2 0.7 %shard_map.65 = (f32[9,16,128]{2,1,0:T(8,128)S(1)}, f32[9,16,128]{2,1,0:T(8,128)S(1)}, f32[9,16,128]{2,1,0:T(8,128)S(1)}, f32[9,16,128]{2,1,0:T(8,128)S(1)}, f32...) custom-call(f32[128,16,128]{2,1,0:T(8,128)S(1)} %copy-done.2, ...), custom_call_target="tpu_custom_call" | custom-call | flops 100000000 | tf_op jit(solution)/shard_map/pallas_call | solution.py:184
  1.9 1.3 %collective-permute-start = (f32[4,7,16,128]{3,2,1,0:T(8,128)S(1)}, f32[4,7,16,128]{3,2,1,0:T(8,128)S(1)}, u32[]{:S(2)}, u32[]{:S(2)}) collective-permute-start(f32[4,7,16,128]{3,2,1,0:T(8,128)S(1)} %get-tuple-element.39), channel_id=1, source_target_pairs={{0,4},{4,0},{8,12},{12,8},{16,20},{20,16},{24,28},{28,24},{1,5},{5... | collective-permute-start | bytes 688136 | tf_op jit(solution)/shard_map/ppermute | solution.py:175
  3.3 0.1 collective-permute-start.10
  3.3 2.3 %collective-permute-start.11 = (f32[9,16,128]{2,1,0:T(8,128)S(1)}, f32[9,16,128]{2,1,0:T(8,128)S(1)}, u32[]{:S(2)}, u32[]{:S(2)}) collective-permute-start(f32[9,16,128]{2,1,0:T(8,128)S(1)} %get-tuple-element.54), channel_id=1, source_target_pairs={{0,20},{4,16},{8,28},{12,24},{16,4},{20,0},{24,12},{28,8},{1,21},{... | collective-permute-start | bytes 221192 | tf_op jit(solution)/shard_map/ppermute | solution.py:175
  5.6 0.2 collective-permute-start.12
  5.7 2.2 %collective-permute-start.13 = (f32[9,16,128]{2,1,0:T(8,128)S(1)}, f32[9,16,128]{2,1,0:T(8,128)S(1)}, u32[]{:S(2)}, u32[]{:S(2)}) collective-permute-start(f32[9,16,128]{2,1,0:T(8,128)S(1)} %get-tuple-element.56), channel_id=1, source_target_pairs={{0,28},{4,24},{8,20},{12,16},{16,12},{20,8},{24,4},{28,0},{1,29},{... | collective-permute-start | bytes 221192 | tf_op jit(solution)/shard_map/ppermute | solution.py:175
  8.0 0.0 collective-permute-done.10.refs_4_
  8.0 0.2 collective-permute-start.7
  8.2 3.3 %collective-permute-done.11.refs_5_ = f32[9,16,128]{2,1,0:T(8,128)S(1)} collective-permute-done((f32[9,16,128]{2,1,0:T(8,128)S(1)}, f32[9,16,128]{2,1,0:T(8,128)S(1)}, u32[]{:S(2)}, u32[]{:S(2)}) %collective-permute-start.11) | collective-permute-done | bytes 73760 | tf_op jit(solution)/shard_map/ppermute | solution.py:175
  11.5 5.7 %collective-permute-start.8 = (f32[9,16,128]{2,1,0:T(8,128)S(1)}, f32[9,16,128]{2,1,0:T(8,128)S(1)}, u32[]{:S(2)}, u32[]{:S(2)}) collective-permute-start(f32[9,16,128]{2,1,0:T(8,128)S(1)} %get-tuple-element.51), channel_id=1, source_target_pairs={{0,8},{4,12},{8,0},{12,4},{16,24},{20,28},{24,16},{28,20},{1,9},{5... | collective-permute-start | bytes 221192 | tf_op jit(solution)/shard_map/ppermute | solution.py:175
  17.2 0.0 collective-permute-done.came.refs_1_
  17.2 1.1 %collective-permute-start.9 = (f32[9,16,128]{2,1,0:T(8,128)S(1)}, f32[9,16,128]{2,1,0:T(8,128)S(1)}, u32[]{:S(2)}, u32[]{:S(2)}) collective-permute-start(f32[9,16,128]{2,1,0:T(8,128)S(1)} %get-tuple-element.52), channel_id=1, source_target_pairs={{0,12},{4,8},{8,4},{12,0},{16,28},{20,24},{24,20},{28,16},{1,13},{... | collective-permute-start | bytes 221192 | tf_op jit(solution)/shard_map/ppermute | solution.py:175
  18.4 0.0 collective-permute-done.12.refs_6_
  18.4 1.5 %collective-permute-start.1 = (f32[2,7,16,128]{3,2,1,0:T(8,128)S(1)}, f32[2,7,16,128]{3,2,1,0:T(8,128)S(1)}, u32[]{:S(2)}, u32[]{:S(2)}) collective-permute-start(f32[2,7,16,128]{3,2,1,0:T(8,128)S(1)} %get-tuple-element.40), channel_id=1, source_target_pairs={{0,8},{4,12},{8,0},{12,4},{16,24},{20,28},{24,16},{28,20},{1,9},{5... | collective-permute-start | bytes 344072 | tf_op jit(solution)/shard_map/ppermute | solution.py:175
  19.9 0.0 collective-permute-done.13.refs_7_
  19.9 0.0 collective-permute-done.7.refs_1_
  19.9 0.0 collective-permute-done.8.refs_2_
  19.9 1.7 %collective-permute-done.9.refs_3_ = f32[9,16,128]{2,1,0:T(8,128)S(1)} collective-permute-done((f32[9,16,128]{2,1,0:T(8,128)S(1)}, f32[9,16,128]{2,1,0:T(8,128)S(1)}, u32[]{:S(2)}, u32[]{:S(2)}) %collective-permute-start.9) | collective-permute-done | bytes 73760 | tf_op jit(solution)/shard_map/ppermute | solution.py:175
  21.6 0.3 shard_map.69
  22.0 0.0 copy-start
  22.0 2.8 %collective-permute-start.14 = (f32[9,32,128]{2,1,0:T(8,128)S(1)}, f32[9,32,128]{2,1,0:T(8,128)S(1)}, u32[]{:S(2)}, u32[]{:S(2)}) collective-permute-start(f32[9,32,128]{2,1,0:T(8,128)S(1)} %get-tuple-element.58), channel_id=1, source_target_pairs={{0,1},{1,0},{2,3},{3,2},{4,5},{5,4},{6,7},{7,6},{8,9},{9,8},{10,11... | collective-permute-start | bytes 442376 | tf_op jit(solution)/shard_map/ppermute | solution.py:175
  24.8 0.0 collective-permute-start.2
  24.8 2.5 %collective-permute-start.3 = (f32[2,7,16,128]{3,2,1,0:T(8,128)S(1)}, f32[2,7,16,128]{3,2,1,0:T(8,128)S(1)}, u32[]{:S(2)}, u32[]{:S(2)}) collective-permute-start(f32[2,7,16,128]{3,2,1,0:T(8,128)S(1)} %get-tuple-element.42), channel_id=1, source_target_pairs={{0,24},{4,28},{8,16},{12,20},{16,8},{20,12},{24,0},{28,4},{1,25},{... | collective-permute-start | bytes 344072 | tf_op jit(solution)/shard_map/ppermute | solution.py:175
  27.2 1.2 %collective-permute-start.15 = (f32[9,32,128]{2,1,0:T(8,128)S(1)}, f32[9,32,128]{2,1,0:T(8,128)S(1)}, u32[]{:S(2)}, u32[]{:S(2)}) collective-permute-start(f32[9,32,128]{2,1,0:T(8,128)S(1)} %get-tuple-element.61), channel_id=1, source_target_pairs={{0,2},{1,3},{2,0},{3,1},{4,6},{5,7},{6,4},{7,5},{8,10},{9,11},{10,... | collective-permute-start | bytes 442376 | tf_op jit(solution)/shard_map/ppermute | solution.py:175
  28.4 0.0 collective-permute-done.1.refs_2_
  28.4 1.1 %collective-permute-start.16 = (f32[9,32,128]{2,1,0:T(8,128)S(1)}, f32[9,32,128]{2,1,0:T(8,128)S(1)}, u32[]{:S(2)}, u32[]{:S(2)}) collective-permute-start(f32[9,32,128]{2,1,0:T(8,128)S(1)} %get-tuple-element.62), channel_id=1, source_target_pairs={{0,3},{1,2},{2,1},{3,0},{4,7},{5,6},{6,5},{7,4},{8,11},{9,10},{10,... | collective-permute-start | bytes 442376 | tf_op jit(solution)/shard_map/ppermute | solution.py:175
  29.5 2.8 %collective-permute-done.2.refs_3_ = f32[2,7,16,128]{3,2,1,0:T(8,128)S(1)} collective-permute-done((f32[2,7,16,128]{3,2,1,0:T(8,128)S(1)}, f32[2,7,16,128]{3,2,1,0:T(8,128)S(1)}, u32[]{:S(2)}, u32[]{:S(2)}) %collective-permute-start.2) | collective-permute-done | bytes 114720 | tf_op jit(solution)/shard_map/ppermute | solution.py:175
  32.3 5.9 %collective-permute-done.3.refs_4_ = f32[2,7,16,128]{3,2,1,0:T(8,128)S(1)} collective-permute-done((f32[2,7,16,128]{3,2,1,0:T(8,128)S(1)}, f32[2,7,16,128]{3,2,1,0:T(8,128)S(1)}, u32[]{:S(2)}, u32[]{:S(2)}) %collective-permute-start.3) | collective-permute-done | bytes 114720 | tf_op jit(solution)/shard_map/ppermute | solution.py:175
  38.2 0.3 shard_map.67
  38.5 0.5 %collective-permute-start.4 = (f32[7,32,128]{2,1,0:T(8,128)S(1)}, f32[7,32,128]{2,1,0:T(8,128)S(1)}, u32[]{:S(2)}, u32[]{:S(2)}) collective-permute-start(f32[7,32,128]{2,1,0:T(8,128)S(1)} %get-tuple-element.44), channel_id=1, source_target_pairs={{0,1},{1,0},{2,3},{3,2},{4,5},{5,4},{6,7},{7,6},{8,9},{9,8},{10,11... | collective-permute-start | bytes 344072 | tf_op jit(solution)/shard_map/ppermute | solution.py:175
  39.0 1.2 %collective-permute-start.5 = (f32[7,32,128]{2,1,0:T(8,128)S(1)}, f32[7,32,128]{2,1,0:T(8,128)S(1)}, u32[]{:S(2)}, u32[]{:S(2)}) collective-permute-start(f32[7,32,128]{2,1,0:T(8,128)S(1)} %get-tuple-element.47), channel_id=1, source_target_pairs={{0,2},{1,3},{2,0},{3,1},{4,6},{5,7},{6,4},{7,5},{8,10},{9,11},{10,... | collective-permute-start | bytes 344072 | tf_op jit(solution)/shard_map/ppermute | solution.py:175
  40.2 0.0 collective-permute-done.14.refs_1_
  40.2 0.5 %collective-permute-start.6 = (f32[7,32,128]{2,1,0:T(8,128)S(1)}, f32[7,32,128]{2,1,0:T(8,128)S(1)}, u32[]{:S(2)}, u32[]{:S(2)}) collective-permute-start(f32[7,32,128]{2,1,0:T(8,128)S(1)} %get-tuple-element.48), channel_id=1, source_target_pairs={{0,3},{1,2},{2,1},{3,0},{4,7},{5,6},{6,5},{7,4},{8,11},{9,10},{10,... | collective-permute-start | bytes 344072 | tf_op jit(solution)/shard_map/ppermute | solution.py:175
  40.7 0.0 copy-done.1
  40.7 0.0 copy-done
  40.7 0.7 %copy-done.3 = f32[512]{0:T(512)S(1)} copy-done((f32[512]{0:T(512)S(1)}, f32[512]{0:T(512)}, u32[]{:S(2)}) %copy-start.3) | copy-done | bytes 2072
  41.4 0.0 copy-done.4
  41.4 0.4 shard_map.70
  41.8 0.0 collective-permute-done.15.refs_0_
  41.8 0.0 collective-permute-done.16.refs_1_
  41.8 1.1 %shard_map.71.refs_2_ = f32[16,32,512]{2,1,0:T(8,128)} custom-call(bf16[512,512]{1,0:T(8,128)(2,1)S(1)} %copy-done.1, bf16[512,512]{1,0:T(8,128)(2,1)S(1)} %copy-done, f32[9,32,512]{2,1,0:T(8,128)S(1)} %get-tuple-element.59.acc, f32[9,32,512]{2,1,0:T(8,128)S(1)} %get-tuple-element.60.fac, f32[9,32,128]{2,1,0:T(8,128)S(1)} %collective-permute-done.15.refs_0_, ...), custom_call_target="tpu_custom_call" | custom-call | flops 100000000 | tf_op jit(solution)/shard_map/pallas_call | solution.py:217
  42.9 0.0 collective-permute-done.4.refs_1_
  43.0 0.4 shard_map.68
  43.3 0.3 collective-permute-done.5.refs_0_
  43.6 2.7 %collective-permute-done.6.refs_1_ = f32[7,32,128]{2,1,0:T(8,128)S(1)} collective-permute-done((f32[7,32,128]{2,1,0:T(8,128)S(1)}, f32[7,32,128]{2,1,0:T(8,128)S(1)}, u32[]{:S(2)}, u32[]{:S(2)}) %collective-permute-start.6) | collective-permute-done | bytes 114720 | tf_op jit(solution)/shard_map/ppermute | solution.py:175
  46.3 1.1 %shard_map.72 = f32[16,32,512]{2,1,0:T(8,128)} custom-call(bf16[512,512]{1,0:T(8,128)(2,1)S(1)} %copy-done.1, bf16[512,512]{1,0:T(8,128)(2,1)S(1)} %copy-done, f32[7,32,512]{2,1,0:T(8,128)S(1)} %get-tuple-element.45.acc, f32[7,32,512]{2,1,0:T(8,128)S(1)} %get-tuple-element.46.fac, ...), custom_call_target="tpu_custom_call", output_to_operand_aliasing={{}: (6, {})} | custom-call | flops 100000000 | tf_op jit(solution)/shard_map/pallas_call | solution.py:217
  (7 shorter events, 0.0 us)
Async XLA Ops:
  0.0 1.2 %copy-start.2 = (f32[128,16,128]{2,1,0:T(8,128)S(1)}, f32[128,16,128]{2,1,0:T(8,128)}, u32[]{:S(2)}) copy-start(f32[128,16,128]{2,1,0:T(8,128)} %t_ref.1) | copy-start | bytes 3145732
  1.9 15.3 %collective-permute-start = (f32[4,7,16,128]{3,2,1,0:T(8,128)S(1)}, f32[4,7,16,128]{3,2,1,0:T(8,128)S(1)}, u32[]{:S(2)}, u32[]{:S(2)}) collective-permute-start(f32[4,7,16,128]{3,2,1,0:T(8,128)S(1)} %get-tuple-element.39), channel_id=1, source_target_pairs={{0,4},{4,0},{8,12},{12,8},{16,20},{20,16},{24,28},{28,24},{1,5},{5... | collective-permute-start | bytes 688136 | tf_op jit(solution)/shard_map/ppermute | solution.py:175
  3.3 4.7 %collective-permute-start.10 = (f32[9,16,128]{2,1,0:T(8,128)S(1)}, f32[9,16,128]{2,1,0:T(8,128)S(1)}, u32[]{:S(2)}, u32[]{:S(2)}) collective-permute-start(f32[9,16,128]{2,1,0:T(8,128)S(1)} %get-tuple-element.53), channel_id=1, source_target_pairs={{0,16},{4,20},{8,24},{12,28},{16,0},{20,4},{24,8},{28,12},{1,17},{... | collective-permute-start | bytes 221192 | tf_op jit(solution)/shard_map/ppermute | solution.py:175
  3.3 8.2 %collective-permute-start.11 = (f32[9,16,128]{2,1,0:T(8,128)S(1)}, f32[9,16,128]{2,1,0:T(8,128)S(1)}, u32[]{:S(2)}, u32[]{:S(2)}) collective-permute-start(f32[9,16,128]{2,1,0:T(8,128)S(1)} %get-tuple-element.54), channel_id=1, source_target_pairs={{0,20},{4,16},{8,28},{12,24},{16,4},{20,0},{24,12},{28,8},{1,21},{... | collective-permute-start | bytes 221192 | tf_op jit(solution)/shard_map/ppermute | solution.py:175
  5.6 12.8 %collective-permute-start.12 = (f32[9,16,128]{2,1,0:T(8,128)S(1)}, f32[9,16,128]{2,1,0:T(8,128)S(1)}, u32[]{:S(2)}, u32[]{:S(2)}) collective-permute-start(f32[9,16,128]{2,1,0:T(8,128)S(1)} %get-tuple-element.55), channel_id=1, source_target_pairs={{0,24},{4,28},{8,16},{12,20},{16,8},{20,12},{24,0},{28,4},{1,25},{... | collective-permute-start | bytes 221192 | tf_op jit(solution)/shard_map/ppermute | solution.py:175
  5.7 14.2 %collective-permute-start.13 = (f32[9,16,128]{2,1,0:T(8,128)S(1)}, f32[9,16,128]{2,1,0:T(8,128)S(1)}, u32[]{:S(2)}, u32[]{:S(2)}) collective-permute-start(f32[9,16,128]{2,1,0:T(8,128)S(1)} %get-tuple-element.56), channel_id=1, source_target_pairs={{0,28},{4,24},{8,20},{12,16},{16,12},{20,8},{24,4},{28,0},{1,29},{... | collective-permute-start | bytes 221192 | tf_op jit(solution)/shard_map/ppermute | solution.py:175
  8.0 11.9 %collective-permute-start.7 = (f32[9,16,128]{2,1,0:T(8,128)S(1)}, f32[9,16,128]{2,1,0:T(8,128)S(1)}, u32[]{:S(2)}, u32[]{:S(2)}) collective-permute-start(f32[9,16,128]{2,1,0:T(8,128)S(1)} %get-tuple-element.50), channel_id=1, source_target_pairs={{0,4},{4,0},{8,12},{12,8},{16,20},{20,16},{24,28},{28,24},{1,5},{5... | collective-permute-start | bytes 221192 | tf_op jit(solution)/shard_map/ppermute | solution.py:175
  11.5 8.4 %collective-permute-start.8 = (f32[9,16,128]{2,1,0:T(8,128)S(1)}, f32[9,16,128]{2,1,0:T(8,128)S(1)}, u32[]{:S(2)}, u32[]{:S(2)}) collective-permute-start(f32[9,16,128]{2,1,0:T(8,128)S(1)} %get-tuple-element.51), channel_id=1, source_target_pairs={{0,8},{4,12},{8,0},{12,4},{16,24},{20,28},{24,16},{28,20},{1,9},{5... | collective-permute-start | bytes 221192 | tf_op jit(solution)/shard_map/ppermute | solution.py:175
  17.2 4.4 %collective-permute-start.9 = (f32[9,16,128]{2,1,0:T(8,128)S(1)}, f32[9,16,128]{2,1,0:T(8,128)S(1)}, u32[]{:S(2)}, u32[]{:S(2)}) collective-permute-start(f32[9,16,128]{2,1,0:T(8,128)S(1)} %get-tuple-element.52), channel_id=1, source_target_pairs={{0,12},{4,8},{8,4},{12,0},{16,28},{20,24},{24,20},{28,16},{1,13},{... | collective-permute-start | bytes 221192 | tf_op jit(solution)/shard_map/ppermute | solution.py:175
  18.4 10.1 %collective-permute-start.1 = (f32[2,7,16,128]{3,2,1,0:T(8,128)S(1)}, f32[2,7,16,128]{3,2,1,0:T(8,128)S(1)}, u32[]{:S(2)}, u32[]{:S(2)}) collective-permute-start(f32[2,7,16,128]{3,2,1,0:T(8,128)S(1)} %get-tuple-element.40), channel_id=1, source_target_pairs={{0,8},{4,12},{8,0},{12,4},{16,24},{20,28},{24,16},{28,20},{1,9},{5... | collective-permute-start | bytes 344072 | tf_op jit(solution)/shard_map/ppermute | solution.py:175
  21.6 19.0 %copy-start.1 = (bf16[512,512]{1,0:T(8,128)(2,1)S(1)}, bf16[512,512]{1,0:T(8,128)(2,1)}, u32[]{:S(2)}) copy-start(bf16[512,512]{1,0:T(8,128)(2,1)} %constant.5.clone.hh_ref) | copy-start | bytes 1572868
  22.0 18.7 %copy-start = (bf16[512,512]{1,0:T(8,128)(2,1)S(1)}, bf16[512,512]{1,0:T(8,128)(2,1)}, u32[]{:S(2)}) copy-start(bf16[512,512]{1,0:T(8,128)(2,1)} %constant.4.clone.hl_ref) | copy-start | bytes 1572868
  22.0 18.2 %collective-permute-start.14 = (f32[9,32,128]{2,1,0:T(8,128)S(1)}, f32[9,32,128]{2,1,0:T(8,128)S(1)}, u32[]{:S(2)}, u32[]{:S(2)}) collective-permute-start(f32[9,32,128]{2,1,0:T(8,128)S(1)} %get-tuple-element.58), channel_id=1, source_target_pairs={{0,1},{1,0},{2,3},{3,2},{4,5},{5,4},{6,7},{7,6},{8,9},{9,8},{10,11... | collective-permute-start | bytes 442376 | tf_op jit(solution)/shard_map/ppermute | solution.py:175
  24.8 7.5 %collective-permute-start.2 = (f32[2,7,16,128]{3,2,1,0:T(8,128)S(1)}, f32[2,7,16,128]{3,2,1,0:T(8,128)S(1)}, u32[]{:S(2)}, u32[]{:S(2)}) collective-permute-start(f32[2,7,16,128]{3,2,1,0:T(8,128)S(1)} %get-tuple-element.41), channel_id=1, source_target_pairs={{0,16},{4,20},{8,24},{12,28},{16,0},{20,4},{24,8},{28,12},{1,17},{... | collective-permute-start | bytes 344072 | tf_op jit(solution)/shard_map/ppermute | solution.py:175
  24.8 13.4 %collective-permute-start.3 = (f32[2,7,16,128]{3,2,1,0:T(8,128)S(1)}, f32[2,7,16,128]{3,2,1,0:T(8,128)S(1)}, u32[]{:S(2)}, u32[]{:S(2)}) collective-permute-start(f32[2,7,16,128]{3,2,1,0:T(8,128)S(1)} %get-tuple-element.42), channel_id=1, source_target_pairs={{0,24},{4,28},{8,16},{12,20},{16,8},{20,12},{24,0},{28,4},{1,25},{... | collective-permute-start | bytes 344072 | tf_op jit(solution)/shard_map/ppermute | solution.py:175
  27.2 14.6 %collective-permute-start.15 = (f32[9,32,128]{2,1,0:T(8,128)S(1)}, f32[9,32,128]{2,1,0:T(8,128)S(1)}, u32[]{:S(2)}, u32[]{:S(2)}) collective-permute-start(f32[9,32,128]{2,1,0:T(8,128)S(1)} %get-tuple-element.61), channel_id=1, source_target_pairs={{0,2},{1,3},{2,0},{3,1},{4,6},{5,7},{6,4},{7,5},{8,10},{9,11},{10,... | collective-permute-start | bytes 442376 | tf_op jit(solution)/shard_map/ppermute | solution.py:175
  28.4 13.3 %collective-permute-start.16 = (f32[9,32,128]{2,1,0:T(8,128)S(1)}, f32[9,32,128]{2,1,0:T(8,128)S(1)}, u32[]{:S(2)}, u32[]{:S(2)}) collective-permute-start(f32[9,32,128]{2,1,0:T(8,128)S(1)} %get-tuple-element.62), channel_id=1, source_target_pairs={{0,3},{1,2},{2,1},{3,0},{4,7},{5,6},{6,5},{7,4},{8,11},{9,10},{10,... | collective-permute-start | bytes 442376 | tf_op jit(solution)/shard_map/ppermute | solution.py:175
  38.5 4.5 %collective-permute-start.4 = (f32[7,32,128]{2,1,0:T(8,128)S(1)}, f32[7,32,128]{2,1,0:T(8,128)S(1)}, u32[]{:S(2)}, u32[]{:S(2)}) collective-permute-start(f32[7,32,128]{2,1,0:T(8,128)S(1)} %get-tuple-element.44), channel_id=1, source_target_pairs={{0,1},{1,0},{2,3},{3,2},{4,5},{5,4},{6,7},{7,6},{8,9},{9,8},{10,11... | collective-permute-start | bytes 344072 | tf_op jit(solution)/shard_map/ppermute | solution.py:175
  39.0 4.6 %collective-permute-start.5 = (f32[7,32,128]{2,1,0:T(8,128)S(1)}, f32[7,32,128]{2,1,0:T(8,128)S(1)}, u32[]{:S(2)}, u32[]{:S(2)}) collective-permute-start(f32[7,32,128]{2,1,0:T(8,128)S(1)} %get-tuple-element.47), channel_id=1, source_target_pairs={{0,2},{1,3},{2,0},{3,1},{4,6},{5,7},{6,4},{7,5},{8,10},{9,11},{10,... | collective-permute-start | bytes 344072 | tf_op jit(solution)/shard_map/ppermute | solution.py:175
  40.2 6.1 %collective-permute-start.6 = (f32[7,32,128]{2,1,0:T(8,128)S(1)}, f32[7,32,128]{2,1,0:T(8,128)S(1)}, u32[]{:S(2)}, u32[]{:S(2)}) collective-permute-start(f32[7,32,128]{2,1,0:T(8,128)S(1)} %get-tuple-element.48), channel_id=1, source_target_pairs={{0,3},{1,2},{2,1},{3,0},{4,7},{5,6},{6,5},{7,4},{8,11},{9,10},{10,... | collective-permute-start | bytes 344072 | tf_op jit(solution)/shard_map/ppermute | solution.py:175
  40.7 0.7 %copy-start.3 = (f32[512]{0:T(512)S(1)}, f32[512]{0:T(512)}, u32[]{:S(2)}) copy-start(f32[512]{0:T(512)} %param.9) | copy-start | bytes 6148
  40.7 0.7 %copy-start.4 = (f32[128]{0:T(128)S(1)}, f32[128]{0:T(128)}, u32[]{:S(2)}) copy-start(f32[128]{0:T(128)} %param.7) | copy-start | bytes 1540
  40.7 0.7 %copy-start.5 = (f32[128]{0:T(128)S(1)}, f32[128]{0:T(128)}, u32[]{:S(2)}) copy-start(f32[128]{0:T(128)} %param.8) | copy-start | bytes 1540

commit v3 on v2

--- a/solution.py
+++ b/solution.py
@@ -96,8 +96,8 @@
 
 def join(keep, came, *outs):
     for h, o in enumerate(outs):
-        o[0] = keep[h + 1]
-        o[1] = came[h + 1]
+        o[0] = keep[h]
+        o[1] = came[h]
 
 
 def y_modes(places, cols, hh_ref, hl_ref, *refs):
@@ -107,7 +107,7 @@
     for k in range(0, s, 2):
         ks = range(k, min(k + 2, s))
         right = jnp.concatenate(
-            [jnp.concatenate([pieces[i][q] if at is None else pieces[i][at, q] for i, at in places], axis=0) for q in ks], axis=1)
+            [jnp.concatenate([pieces[i][off + q] if at is None else pieces[i][at, off + q] for i, at, off in places], axis=0) for q in ks], axis=1)
         res = product(left, halves(right))
         for i, q in enumerate(ks):
             for e in range(cols):
@@ -162,7 +162,6 @@
         ny, nz = by * rows, bz * cols
         bx, bk = nx // rows, ny // cols
         half = cols // 2
-        far, near = range(rows // 2, rows), range(1, rows // 2)
         sizes = [w * bx // 16 for w in SPLIT]
         starts = [sum(sizes[:j]) for j in range(len(sizes))]
         chunks = list(zip(starts, sizes))
@@ -179,30 +178,25 @@
             10**9, [])()
         (l0, s0), (l1, s1) = chunks
         deep = rows // 2
-        plan = [[(d, l0, s0)] for d in range(rows)]
-        plan += [[(2 * h + 1, l1, s1) for h in range(deep)], [(2 * h, l1, s1) for h in range(deep)]]
+        hs = range(1, deep)
+        plan = [[(d, 0, bx)] for d in range(2)] + [[(d, l0, s0)] for d in range(2, rows)]
+        plan += [[(2 * h + 1, l1, s1) for h in hs], [(2 * h, l1, s1) for h in hs]]
         u = call(
-            functools.partial(x_modes, plan, bx), [shape(s0, by, bz)] * rows + [shape(deep, s1, by, bz)] * 2, 10**8, [VMEM] * 3,
-        )(tracer, xh, xl)
-        got = {0: u[0]}
-        for d in far:
-            got[d] = send(u[d], "row", d, rows)
-        for d in near:
-            got[d] = send(u[d], "row", d, rows)
+            functools.partial(x_modes, plan, bx),
+            [shape(bx, by, bz)] * 2 + [shape(s0, by, bz)] * (rows - 2) + [shape(len(hs), s1, by, bz)] * 2, 10**8,
+            [VMEM] * 3)(tracer, xh, xl)
+        got = [u[0]] + [send(u[d], "row", d, rows) for d in range(1, rows)]
         keep = u[-1]
         came = send(u[-2], "row", 1, rows)
-        both = call(join, [shape(2, s1, by, bz)] * (deep - 1), 10**6, [VMEM] * 2)(keep, came)
-        full = [send(both[h - 1], "row", 2 * h, rows) for h in range(1, deep)]
+        both = call(join, [shape(2, s1, by, bz)] * len(hs), 10**6, [VMEM] * 2)(keep, came)
+        full = [send(v, "row", 2 * h, rows) for h, v in zip(hs, both)]
+        arrived = [(got, [(d, None, 0) for d in range(rows)]),
+                   (got[:2] + full, [(d, None, l1) for d in range(2)] + [(2 + h, i, 0) for h in range(len(hs)) for i in range(2)])]
 
         sx, sy, sz = symbol_x.reshape(1, nx), symbol_y.reshape(1, ny), symbol_z.reshape(1, nz)
         out = None
         for j, (lo, s) in enumerate(chunks):
-            if j == 0:
-                pieces = [got[d] for d in range(rows)]
-                places = [(d, None) for d in range(rows)]
-            else:
-                pieces = [keep, came] + full
-                places = [(0, 0), (1, 0)] + [(2 + h, i) for h in range(deep - 1) for i in range(2)]
+            pieces, places = arrived[j]
             w = call(
                 functools.partial(y_modes, places, cols), [shape(s, bk, bz)] * cols,
                 10**8, [VMEM] * (2 + len(pieces)))(yh, yl, *pieces)

time: 47.5 us -> 45.9 us (0.966)
  the two profiles are of different devices: /device:TPU:17 before, /device:TPU:0 now
where the time goes in v3:
time: 45.9 us; the launch traced here: 45.7 us
  starting transfers between devices  24.8 us (54%)
  waiting for transfers between devices  14.7 us (32%)
  Pallas kernels  4.77 us (10%)
  local copies, waits for them, and re-layouts  1.4 us (3%)
    ppermute x17, starting transfers between devices, send(): return lax.ppermute(value, axis, [(i, i ^ d) for i in range(n)])  24.8 us
    ppermute x17, waiting for transfers between devices, send(): return lax.ppermute(value, axis, [(i, i ^ d) for i in range(n)])  14.7 us
    pallas_call x2, Pallas kernels, per_device(): call(functools.partial(z_last, lo, half, GROUP), shape(bx, bk, nz), 10 **...  2.19 us
    unnamed x12, local copies, waits for them, and re-layouts  1.4 us
  transfers between devices with their start and end apart: 17, of which 6 were waited for; matrix products, arithmetic and copies ran while one was open for 0% of the time, Pallas kernels for 6%

profile of v3, /device:TPU:0, one launch (start us, length us, event | category | flops | bytes accessed | tf_op | source)
XLA Modules:
  0.0 45.7 jit_solution(11802866912149637973)
XLA Ops:
  0.0 0.5 %shard_map.64 = (bf16[128,128]{1,0:T(8,128)(2,1)S(1)}, bf16[128,128]{1,0:T(8,128)(2,1)S(1)}, bf16[128,128]{1,0:T(8,128)(2,1)S(1)}, bf16[128,128]{1,0:T(8,128)(2,1)S(1)}) custom-call(), custom_call_target="tpu_custom_call" | custom-call | flops 1000000000 | tf_op jit(solution)/shard_map/pallas_call | solution.py:176
  0.5 0.7 %copy-done.2 = f32[128,16,128]{2,1,0:T(8,128)S(1)} copy-done((f32[128,16,128]{2,1,0:T(8,128)S(1)}, f32[128,16,128]{2,1,0:T(8,128)}, u32[]{:S(2)}) %copy-start.2) | copy-done | bytes 1048600
  1.2 0.7 %shard_map.65 = (f32[16,16,128]{2,1,0:T(8,128)S(1)}, f32[16,16,128]{2,1,0:T(8,128)S(1)}, f32[9,16,128]{2,1,0:T(8,128)S(1)}, f32[9,16,128]{2,1,0:T(8,128)S(1)}, f...) custom-call(f32[128,16,128]{2,1,0:T(8,128)S(1)} %copy-done.2, ...), custom_call_target="tpu_custom_call" | custom-call | flops 100000000 | tf_op jit(solution)/shard_map/pallas_call | solution.py:184
  1.9 3.1 %collective-permute-start.1 = (f32[3,7,16,128]{3,2,1,0:T(8,128)S(1)}, f32[3,7,16,128]{3,2,1,0:T(8,128)S(1)}, u32[]{:S(2)}, u32[]{:S(2)}) collective-permute-start(f32[3,7,16,128]{3,2,1,0:T(8,128)S(1)} %get-tuple-element.41), channel_id=1, source_target_pairs={{0,4},{4,0},{8,12},{12,8},{16,20},{20,16},{24,28},{28,24},{1,5},{5... | collective-permute-start | bytes 516104 | tf_op jit(solution)/shard_map/ppermute | solution.py:174
  5.0 2.6 %collective-permute-start.10 = (f32[9,16,128]{2,1,0:T(8,128)S(1)}, f32[9,16,128]{2,1,0:T(8,128)S(1)}, u32[]{:S(2)}, u32[]{:S(2)}) collective-permute-start(f32[9,16,128]{2,1,0:T(8,128)S(1)} %get-tuple-element.53), channel_id=1, source_target_pairs={{0,16},{4,20},{8,24},{12,28},{16,0},{20,4},{24,8},{28,12},{1,17},{... | collective-permute-start | bytes 221192 | tf_op jit(solution)/shard_map/ppermute | solution.py:174
  7.6 0.0 collective-permute-start.11
  7.6 1.8 %collective-permute-start = (f32[16,16,128]{2,1,0:T(8,128)S(1)}, f32[16,16,128]{2,1,0:T(8,128)S(1)}, u32[]{:S(2)}, u32[]{:S(2)}) collective-permute-start(f32[16,16,128]{2,1,0:T(8,128)S(1)} %get-tuple-element.39), channel_id=1, source_target_pairs={{0,4},{4,0},{8,12},{12,8},{16,20},{20,16},{24,28},{28,24},{1,5},{5... | collective-permute-start | bytes 393224 | tf_op jit(solution)/shard_map/ppermute | solution.py:174
  9.4 3.6 %collective-permute-start.12 = (f32[9,16,128]{2,1,0:T(8,128)S(1)}, f32[9,16,128]{2,1,0:T(8,128)S(1)}, u32[]{:S(2)}, u32[]{:S(2)}) collective-permute-start(f32[9,16,128]{2,1,0:T(8,128)S(1)} %get-tuple-element.55), channel_id=1, source_target_pairs={{0,24},{4,28},{8,16},{12,20},{16,8},{20,12},{24,0},{28,4},{1,25},{... | collective-permute-start | bytes 221192 | tf_op jit(solution)/shard_map/ppermute | solution.py:174
  13.0 0.0 collective-permute-done.10.refs_4_
  13.0 4.2 %collective-permute-start.13 = (f32[9,16,128]{2,1,0:T(8,128)S(1)}, f32[9,16,128]{2,1,0:T(8,128)S(1)}, u32[]{:S(2)}, u32[]{:S(2)}) collective-permute-start(f32[9,16,128]{2,1,0:T(8,128)S(1)} %get-tuple-element.56), channel_id=1, source_target_pairs={{0,28},{4,24},{8,20},{12,16},{16,12},{20,8},{24,4},{28,0},{1,29},{... | collective-permute-start | bytes 221192 | tf_op jit(solution)/shard_map/ppermute | solution.py:174
  17.2 0.7 %collective-permute-done.11.refs_5_ = f32[9,16,128]{2,1,0:T(8,128)S(1)} collective-permute-done((f32[9,16,128]{2,1,0:T(8,128)S(1)}, f32[9,16,128]{2,1,0:T(8,128)S(1)}, u32[]{:S(2)}, u32[]{:S(2)}) %collective-permute-start.11) | collective-permute-done | bytes 73760 | tf_op jit(solution)/shard_map/ppermute | solution.py:174
  17.9 0.0 collective-permute-start.8
  17.9 0.0 collective-permute-done.1.came
  17.9 2.2 %collective-permute-start.9 = (f32[9,16,128]{2,1,0:T(8,128)S(1)}, f32[9,16,128]{2,1,0:T(8,128)S(1)}, u32[]{:S(2)}, u32[]{:S(2)}) collective-permute-start(f32[9,16,128]{2,1,0:T(8,128)S(1)} %get-tuple-element.52), channel_id=1, source_target_pairs={{0,12},{4,8},{8,4},{12,0},{16,28},{20,24},{24,20},{28,16},{1,13},{... | collective-permute-start | bytes 221192 | tf_op jit(solution)/shard_map/ppermute | solution.py:174
  20.1 0.0 collective-permute-done.12.refs_6_
  20.1 0.1 collective-permute-start.2
  20.2 0.0 collective-permute-done.13.refs_7_
  20.3 2.8 %collective-permute-done.8.refs_2_ = f32[9,16,128]{2,1,0:T(8,128)S(1)} collective-permute-done((f32[9,16,128]{2,1,0:T(8,128)S(1)}, f32[9,16,128]{2,1,0:T(8,128)S(1)}, u32[]{:S(2)}, u32[]{:S(2)}) %collective-permute-start.8) | collective-permute-done | bytes 73760 | tf_op jit(solution)/shard_map/ppermute | solution.py:174
  23.0 1.5 %collective-permute-done.9.refs_3_ = f32[9,16,128]{2,1,0:T(8,128)S(1)} collective-permute-done((f32[9,16,128]{2,1,0:T(8,128)S(1)}, f32[9,16,128]{2,1,0:T(8,128)S(1)}, u32[]{:S(2)}, u32[]{:S(2)}) %collective-permute-start.9) | collective-permute-done | bytes 73760 | tf_op jit(solution)/shard_map/ppermute | solution.py:174
  24.5 0.0 collective-permute-done.refs_1_
  24.5 0.3 shard_map.69
  24.9 0.0 copy-start
  24.9 0.1 collective-permute-start.14
  24.9 1.7 %collective-permute-start.3 = (f32[2,7,16,128]{3,2,1,0:T(8,128)S(1)}, f32[2,7,16,128]{3,2,1,0:T(8,128)S(1)}, u32[]{:S(2)}, u32[]{:S(2)}) collective-permute-start(f32[2,7,16,128]{3,2,1,0:T(8,128)S(1)} %get-tuple-element.43), channel_id=1, source_target_pairs={{0,16},{4,20},{8,24},{12,28},{16,0},{20,4},{24,8},{28,12},{1,17},{... | collective-permute-start | bytes 344072 | tf_op jit(solution)/shard_map/ppermute | solution.py:174
  26.6 2.0 %collective-permute-start.4 = (f32[2,7,16,128]{3,2,1,0:T(8,128)S(1)}, f32[2,7,16,128]{3,2,1,0:T(8,128)S(1)}, u32[]{:S(2)}, u32[]{:S(2)}) collective-permute-start(f32[2,7,16,128]{3,2,1,0:T(8,128)S(1)} %get-tuple-element.44), channel_id=1, source_target_pairs={{0,24},{4,28},{8,16},{12,20},{16,8},{20,12},{24,0},{28,4},{1,25},{... | collective-permute-start | bytes 344072 | tf_op jit(solution)/shard_map/ppermute | solution.py:174
  28.6 1.5 %collective-permute-start.15 = (f32[9,32,128]{2,1,0:T(8,128)S(1)}, f32[9,32,128]{2,1,0:T(8,128)S(1)}, u32[]{:S(2)}, u32[]{:S(2)}) collective-permute-start(f32[9,32,128]{2,1,0:T(8,128)S(1)} %get-tuple-element.61), channel_id=1, source_target_pairs={{0,2},{1,3},{2,0},{3,1},{4,6},{5,7},{6,4},{7,5},{8,10},{9,11},{10,... | collective-permute-start | bytes 442376 | tf_op jit(solution)/shard_map/ppermute | solution.py:174
  30.1 0.0 collective-permute-done.2.refs_2_
  30.1 0.0 collective-permute-start.16
  30.1 6.7 %collective-permute-done.3.refs_3_ = f32[2,7,16,128]{3,2,1,0:T(8,128)S(1)} collective-permute-done((f32[2,7,16,128]{3,2,1,0:T(8,128)S(1)}, f32[2,7,16,128]{3,2,1,0:T(8,128)S(1)}, u32[]{:S(2)}, u32[]{:S(2)}) %collective-permute-start.3) | collective-permute-done | bytes 114720 | tf_op jit(solution)/shard_map/ppermute | solution.py:174
  36.8 0.0 collective-permute-done.4.refs_4_
  36.9 0.3 shard_map.67
  37.2 0.1 collective-permute-start.5
  37.2 1.6 %collective-permute-start.6 = (f32[7,32,128]{2,1,0:T(8,128)S(1)}, f32[7,32,128]{2,1,0:T(8,128)S(1)}, u32[]{:S(2)}, u32[]{:S(2)}) collective-permute-start(f32[7,32,128]{2,1,0:T(8,128)S(1)} %get-tuple-element.49), channel_id=1, source_target_pairs={{0,2},{1,3},{2,0},{3,1},{4,6},{5,7},{6,4},{7,5},{8,10},{9,11},{10,... | collective-permute-start | bytes 344072 | tf_op jit(solution)/shard_map/ppermute | solution.py:174
  38.8 0.0 collective-permute-done.14.refs_1_
  38.8 0.3 collective-permute-start.7
  39.1 0.0 copy-done.1
  39.1 0.0 copy-done
  39.1 0.7 %copy-done.3 = f32[512]{0:T(512)S(1)} copy-done((f32[512]{0:T(512)S(1)}, f32[512]{0:T(512)}, u32[]{:S(2)}) %copy-start.3) | copy-done | bytes 2072
  39.8 0.0 copy-done.4
  39.8 0.4 shard_map.70
  40.2 0.0 collective-permute-done.15.refs_0_
  40.2 0.0 collective-permute-done.16.refs_1_
  40.2 1.1 %shard_map.71.refs_2_ = f32[16,32,512]{2,1,0:T(8,128)} custom-call(bf16[512,512]{1,0:T(8,128)(2,1)S(1)} %copy-done.1, bf16[512,512]{1,0:T(8,128)(2,1)S(1)} %copy-done, f32[9,32,512]{2,1,0:T(8,128)S(1)} %get-tuple-element.59.acc, f32[9,32,512]{2,1,0:T(8,128)S(1)} %get-tuple-element.60.fac, f32[9,32,128]{2,1,0:T(8,128)S(1)} %collective-permute-done.15.refs_0_, ...), custom_call_target="tpu_custom_call" | custom-call | flops 100000000 | tf_op jit(solution)/shard_map/pallas_call | solution.py:211
  41.3 0.0 collective-permute-done.5.refs_1_
  41.3 0.4 shard_map.68
  41.7 1.6 %collective-permute-done.6.refs_0_ = f32[7,32,128]{2,1,0:T(8,128)S(1)} collective-permute-done((f32[7,32,128]{2,1,0:T(8,128)S(1)}, f32[7,32,128]{2,1,0:T(8,128)S(1)}, u32[]{:S(2)}, u32[]{:S(2)}) %collective-permute-start.6) | collective-permute-done | bytes 114720 | tf_op jit(solution)/shard_map/ppermute | solution.py:174
  43.3 1.4 %collective-permute-done.7.refs_1_ = f32[7,32,128]{2,1,0:T(8,128)S(1)} collective-permute-done((f32[7,32,128]{2,1,0:T(8,128)S(1)}, f32[7,32,128]{2,1,0:T(8,128)S(1)}, u32[]{:S(2)}, u32[]{:S(2)}) %collective-permute-start.7) | collective-permute-done | bytes 114720 | tf_op jit(solution)/shard_map/ppermute | solution.py:174
  44.7 1.1 %shard_map.72 = f32[16,32,512]{2,1,0:T(8,128)} custom-call(bf16[512,512]{1,0:T(8,128)(2,1)S(1)} %copy-done.1, bf16[512,512]{1,0:T(8,128)(2,1)S(1)} %copy-done, f32[7,32,512]{2,1,0:T(8,128)S(1)} %get-tuple-element.47.acc, f32[7,32,512]{2,1,0:T(8,128)S(1)} %get-tuple-element.48.fac, ...), custom_call_target="tpu_custom_call", output_to_operand_aliasing={{}: (6, {})} | custom-call | flops 100000000 | tf_op jit(solution)/shard_map/pallas_call | solution.py:211
  (7 shorter events, 0.0 us)
Async XLA Ops:
  0.0 1.2 %copy-start.2 = (f32[128,16,128]{2,1,0:T(8,128)S(1)}, f32[128,16,128]{2,1,0:T(8,128)}, u32[]{:S(2)}) copy-start(f32[128,16,128]{2,1,0:T(8,128)} %t_ref.1) | copy-start | bytes 3145732
  1.9 16.0 %collective-permute-start.1 = (f32[3,7,16,128]{3,2,1,0:T(8,128)S(1)}, f32[3,7,16,128]{3,2,1,0:T(8,128)S(1)}, u32[]{:S(2)}, u32[]{:S(2)}) collective-permute-start(f32[3,7,16,128]{3,2,1,0:T(8,128)S(1)} %get-tuple-element.41), channel_id=1, source_target_pairs={{0,4},{4,0},{8,12},{12,8},{16,20},{20,16},{24,28},{28,24},{1,5},{5... | collective-permute-start | bytes 516104 | tf_op jit(solution)/shard_map/ppermute | solution.py:174
  5.0 8.0 %collective-permute-start.10 = (f32[9,16,128]{2,1,0:T(8,128)S(1)}, f32[9,16,128]{2,1,0:T(8,128)S(1)}, u32[]{:S(2)}, u32[]{:S(2)}) collective-permute-start(f32[9,16,128]{2,1,0:T(8,128)S(1)} %get-tuple-element.53), channel_id=1, source_target_pairs={{0,16},{4,20},{8,24},{12,28},{16,0},{20,4},{24,8},{28,12},{1,17},{... | collective-permute-start | bytes 221192 | tf_op jit(solution)/shard_map/ppermute | solution.py:174
  7.6 10.3 %collective-permute-start.11 = (f32[9,16,128]{2,1,0:T(8,128)S(1)}, f32[9,16,128]{2,1,0:T(8,128)S(1)}, u32[]{:S(2)}, u32[]{:S(2)}) collective-permute-start(f32[9,16,128]{2,1,0:T(8,128)S(1)} %get-tuple-element.54), channel_id=1, source_target_pairs={{0,20},{4,16},{8,28},{12,24},{16,4},{20,0},{24,12},{28,8},{1,21},{... | collective-permute-start | bytes 221192 | tf_op jit(solution)/shard_map/ppermute | solution.py:174
  7.6 16.9 %collective-permute-start = (f32[16,16,128]{2,1,0:T(8,128)S(1)}, f32[16,16,128]{2,1,0:T(8,128)S(1)}, u32[]{:S(2)}, u32[]{:S(2)}) collective-permute-start(f32[16,16,128]{2,1,0:T(8,128)S(1)} %get-tuple-element.39), channel_id=1, source_target_pairs={{0,4},{4,0},{8,12},{12,8},{16,20},{20,16},{24,28},{28,24},{1,5},{5... | collective-permute-start | bytes 393224 | tf_op jit(solution)/shard_map/ppermute | solution.py:174
  9.4 10.7 %collective-permute-start.12 = (f32[9,16,128]{2,1,0:T(8,128)S(1)}, f32[9,16,128]{2,1,0:T(8,128)S(1)}, u32[]{:S(2)}, u32[]{:S(2)}) collective-permute-start(f32[9,16,128]{2,1,0:T(8,128)S(1)} %get-tuple-element.55), channel_id=1, source_target_pairs={{0,24},{4,28},{8,16},{12,20},{16,8},{20,12},{24,0},{28,4},{1,25},{... | collective-permute-start | bytes 221192 | tf_op jit(solution)/shard_map/ppermute | solution.py:174
  13.0 7.3 %collective-permute-start.13 = (f32[9,16,128]{2,1,0:T(8,128)S(1)}, f32[9,16,128]{2,1,0:T(8,128)S(1)}, u32[]{:S(2)}, u32[]{:S(2)}) collective-permute-start(f32[9,16,128]{2,1,0:T(8,128)S(1)} %get-tuple-element.56), channel_id=1, source_target_pairs={{0,28},{4,24},{8,20},{12,16},{16,12},{20,8},{24,4},{28,0},{1,29},{... | collective-permute-start | bytes 221192 | tf_op jit(solution)/shard_map/ppermute | solution.py:174
  17.9 5.1 %collective-permute-start.8 = (f32[9,16,128]{2,1,0:T(8,128)S(1)}, f32[9,16,128]{2,1,0:T(8,128)S(1)}, u32[]{:S(2)}, u32[]{:S(2)}) collective-permute-start(f32[9,16,128]{2,1,0:T(8,128)S(1)} %get-tuple-element.51), channel_id=1, source_target_pairs={{0,8},{4,12},{8,0},{12,4},{16,24},{20,28},{24,16},{28,20},{1,9},{5... | collective-permute-start | bytes 221192 | tf_op jit(solution)/shard_map/ppermute | solution.py:174
  17.9 6.6 %collective-permute-start.9 = (f32[9,16,128]{2,1,0:T(8,128)S(1)}, f32[9,16,128]{2,1,0:T(8,128)S(1)}, u32[]{:S(2)}, u32[]{:S(2)}) collective-permute-start(f32[9,16,128]{2,1,0:T(8,128)S(1)} %get-tuple-element.52), channel_id=1, source_target_pairs={{0,12},{4,8},{8,4},{12,0},{16,28},{20,24},{24,20},{28,16},{1,13},{... | collective-permute-start | bytes 221192 | tf_op jit(solution)/shard_map/ppermute | solution.py:174
  20.1 10.0 %collective-permute-start.2 = (f32[2,7,16,128]{3,2,1,0:T(8,128)S(1)}, f32[2,7,16,128]{3,2,1,0:T(8,128)S(1)}, u32[]{:S(2)}, u32[]{:S(2)}) collective-permute-start(f32[2,7,16,128]{3,2,1,0:T(8,128)S(1)} %get-tuple-element.42), channel_id=1, source_target_pairs={{0,8},{4,12},{8,0},{12,4},{16,24},{20,28},{24,16},{28,20},{1,9},{5... | collective-permute-start | bytes 344072 | tf_op jit(solution)/shard_map/ppermute | solution.py:174
  24.5 14.6 %copy-start.1 = (bf16[512,512]{1,0:T(8,128)(2,1)S(1)}, bf16[512,512]{1,0:T(8,128)(2,1)}, u32[]{:S(2)}) copy-start(bf16[512,512]{1,0:T(8,128)(2,1)} %constant.5.clone.hh_ref) | copy-start | bytes 1572868
  24.9 14.2 %copy-start = (bf16[512,512]{1,0:T(8,128)(2,1)S(1)}, bf16[512,512]{1,0:T(8,128)(2,1)}, u32[]{:S(2)}) copy-start(bf16[512,512]{1,0:T(8,128)(2,1)} %constant.4.clone.hl_ref) | copy-start | bytes 1572868
  24.9 13.9 %collective-permute-start.14 = (f32[9,32,128]{2,1,0:T(8,128)S(1)}, f32[9,32,128]{2,1,0:T(8,128)S(1)}, u32[]{:S(2)}, u32[]{:S(2)}) collective-permute-start(f32[9,32,128]{2,1,0:T(8,128)S(1)} %get-tuple-element.58), channel_id=1, source_target_pairs={{0,1},{1,0},{2,3},{3,2},{4,5},{5,4},{6,7},{7,6},{8,9},{9,8},{10,11... | collective-permute-start | bytes 442376 | tf_op jit(solution)/shard_map/ppermute | solution.py:174
  24.9 11.9 %collective-permute-start.3 = (f32[2,7,16,128]{3,2,1,0:T(8,128)S(1)}, f32[2,7,16,128]{3,2,1,0:T(8,128)S(1)}, u32[]{:S(2)}, u32[]{:S(2)}) collective-permute-start(f32[2,7,16,128]{3,2,1,0:T(8,128)S(1)} %get-tuple-element.43), channel_id=1, source_target_pairs={{0,16},{4,20},{8,24},{12,28},{16,0},{20,4},{24,8},{28,12},{1,17},{... | collective-permute-start | bytes 344072 | tf_op jit(solution)/shard_map/ppermute | solution.py:174
  26.6 10.2 %collective-permute-start.4 = (f32[2,7,16,128]{3,2,1,0:T(8,128)S(1)}, f32[2,7,16,128]{3,2,1,0:T(8,128)S(1)}, u32[]{:S(2)}, u32[]{:S(2)}) collective-permute-start(f32[2,7,16,128]{3,2,1,0:T(8,128)S(1)} %get-tuple-element.44), channel_id=1, source_target_pairs={{0,24},{4,28},{8,16},{12,20},{16,8},{20,12},{24,0},{28,4},{1,25},{... | collective-permute-start | bytes 344072 | tf_op jit(solution)/shard_map/ppermute | solution.py:174
  28.6 11.6 %collective-permute-start.15 = (f32[9,32,128]{2,1,0:T(8,128)S(1)}, f32[9,32,128]{2,1,0:T(8,128)S(1)}, u32[]{:S(2)}, u32[]{:S(2)}) collective-permute-start(f32[9,32,128]{2,1,0:T(8,128)S(1)} %get-tuple-element.61), channel_id=1, source_target_pairs={{0,2},{1,3},{2,0},{3,1},{4,6},{5,7},{6,4},{7,5},{8,10},{9,11},{10,... | collective-permute-start | bytes 442376 | tf_op jit(solution)/shard_map/ppermute | solution.py:174
  30.1 10.1 %collective-permute-start.16 = (f32[9,32,128]{2,1,0:T(8,128)S(1)}, f32[9,32,128]{2,1,0:T(8,128)S(1)}, u32[]{:S(2)}, u32[]{:S(2)}) collective-permute-start(f32[9,32,128]{2,1,0:T(8,128)S(1)} %get-tuple-element.62), channel_id=1, source_target_pairs={{0,3},{1,2},{2,1},{3,0},{4,7},{5,6},{6,5},{7,4},{8,11},{9,10},{10,... | collective-permute-start | bytes 442376 | tf_op jit(solution)/shard_map/ppermute | solution.py:174
  37.2 4.2 %collective-permute-start.5 = (f32[7,32,128]{2,1,0:T(8,128)S(1)}, f32[7,32,128]{2,1,0:T(8,128)S(1)}, u32[]{:S(2)}, u32[]{:S(2)}) collective-permute-start(f32[7,32,128]{2,1,0:T(8,128)S(1)} %get-tuple-element.46), channel_id=1, source_target_pairs={{0,1},{1,0},{2,3},{3,2},{4,5},{5,4},{6,7},{7,6},{8,9},{9,8},{10,11... | collective-permute-start | bytes 344072 | tf_op jit(solution)/shard_map/ppermute | solution.py:174
  37.2 6.1 %collective-permute-start.6 = (f32[7,32,128]{2,1,0:T(8,128)S(1)}, f32[7,32,128]{2,1,0:T(8,128)S(1)}, u32[]{:S(2)}, u32[]{:S(2)}) collective-permute-start(f32[7,32,128]{2,1,0:T(8,128)S(1)} %get-tuple-element.49), channel_id=1, source_target_pairs={{0,2},{1,3},{2,0},{3,1},{4,6},{5,7},{6,4},{7,5},{8,10},{9,11},{10,... | collective-permute-start | bytes 344072 | tf_op jit(solution)/shard_map/ppermute | solution.py:174
  38.8 5.9 %collective-permute-start.7 = (f32[7,32,128]{2,1,0:T(8,128)S(1)}, f32[7,32,128]{2,1,0:T(8,128)S(1)}, u32[]{:S(2)}, u32[]{:S(2)}) collective-permute-start(f32[7,32,128]{2,1,0:T(8,128)S(1)} %get-tuple-element.50), channel_id=1, source_target_pairs={{0,3},{1,2},{2,1},{3,0},{4,7},{5,6},{6,5},{7,4},{8,11},{9,10},{10,... | collective-permute-start | bytes 344072 | tf_op jit(solution)/shard_map/ppermute | solution.py:174
  39.1 0.7 %copy-start.3 = (f32[512]{0:T(512)S(1)}, f32[512]{0:T(512)}, u32[]{:S(2)}) copy-start(f32[512]{0:T(512)} %param.9) | copy-start | bytes 6148
  39.1 0.7 %copy-start.4 = (f32[128]{0:T(128)S(1)}, f32[128]{0:T(128)}, u32[]{:S(2)}) copy-start(f32[128]{0:T(128)} %param.7) | copy-start | bytes 1540
  39.1 0.7 %copy-start.5 = (f32[128]{0:T(128)S(1)}, f32[128]{0:T(128)}, u32[]{:S(2)}) copy-start(f32[128]{0:T(128)} %param.8) | copy-start | bytes 1540
